TPU v7x, 8 devices: a whole 2x2x1 slice. The times are simulated.
8 devices in a mesh: rep: 1 (over z), data: 8 (over y, x, core).
Axes of the slice: x: 2, y: 2, z: 1, core: 2. Of those that a mesh axis runs over, the one named last changes fastest.
Arguments:
- x: bfloat16 [1024, 2048], P(('rep', 'data'))
- adapter_id: int32 [1024], P(('rep', 'data'))
- dout: bfloat16 [1024, 2048], P(('rep', 'data'))
- w_gate: bfloat16 [2048, 8192], replicated
- w_up: bfloat16 [2048, 8192], replicated
- w_down: bfloat16 [8192, 2048], replicated
- a_gate: bfloat16 [256, 2048, 16], P('data')
- b_gate: bfloat16 [256, 16, 8192], P('data')
- a_up: bfloat16 [256, 2048, 16], P('data')
- b_up: bfloat16 [256, 16, 8192], P('data')
- a_down: bfloat16 [256, 8192, 16], P('data')
- b_down: bfloat16 [256, 16, 2048], P('data')
Outputs:
- output 1: bfloat16 [1024, 2048], P(('rep', 'data'))
- output 2: bfloat16 [1024, 2048], P(('rep', 'data'))
- output 3: float32 [256, 2048, 16], P(('rep', 'data'))
- output 4: float32 [256, 16, 8192], P(('rep', 'data'))
- output 5: float32 [256, 2048, 16], P(('rep', 'data'))
- output 6: float32 [256, 16, 8192], P(('rep', 'data'))
- output 7: float32 [256, 8192, 16], P(('rep', 'data'))
- output 8: float32 [256, 16, 2048], P(('rep', 'data'))
All inputs are finite; a program needn't handle non-finite values.
Results may differ from a plain program's by a relative error of at most 0.00149.
Values are sent between devices in bfloat16 or wider.
A program may use at most 1 GiB of HBM per device.

v0:
```python
import functools

import jax
import jax.numpy as jnp
from jax import lax
from jax.experimental import pallas as pl
from jax.experimental.pallas import tpu as pltpu
from jax.sharding import PartitionSpec as P

LORA_ALPHA = 32
TILE = 512
f32 = jnp.float32
bf = jnp.bfloat16


def mm(left, right, ldim=1, rdim=0):
    return lax.dot_general(left, right, (((ldim,), (rdim,)), ((), ())), preferred_element_type=f32)


def rounded(vals):
    return vals.astype(bf).astype(f32)


def keep(vals, ids, rank):
    cols = lax.div(lax.broadcasted_iota(jnp.int32, vals.shape, 1), jnp.int32(rank))
    return jnp.where(cols == ids, vals, 0.0).astype(bf)


def forward_body(rank, scale, ids, x, ag, au, bd, wg, wu, wd, bg, bu, ad, gate_o, up_o, out_o, pg_o, pu_o, pd_o, acc, pd_acc):
    step = pl.program_id(0)

    @pl.when(step == 0)
    def _():
        pg_o[...] = keep(mm(x[...], ag[...], 1, 1), ids[...], rank)
        pu_o[...] = keep(mm(x[...], au[...], 1, 1), ids[...], rank)
        acc[...] = jnp.zeros_like(acc)
        pd_acc[...] = jnp.zeros_like(pd_acc)

    gate = mm(x[...], wg[...]) + rounded(scale * mm(pg_o[...], bg[...]))
    up = mm(x[...], wu[...]) + rounded(scale * mm(pu_o[...], bu[...]))
    gate_o[...] = gate
    up_o[...] = up
    h = (gate * jax.nn.sigmoid(gate) * up).astype(bf)
    acc[...] += mm(h, wd[...])
    pd_acc[...] += mm(h, ad[...], 1, 1)

    @pl.when(step == pl.num_programs(0) - 1)
    def _():
        pd = keep(pd_acc[...], ids[...], rank)
        pd_o[...] = pd
        out_o[...] = (x[...].astype(f32) + acc[...] + rounded(scale * mm(pd, bd[...]))).astype(bf)


def backward_body(rank, scale, ids, dy, ag, au, bd, gate_r, up_r, wg, wu, wd, bg, bu, ad,
                  dg_o, du_o, gad_o, dx_o, qg_o, qu_o, acc, qg_acc, qu_acc, qd_s, qdt_s):
    step = pl.program_id(0)

    @pl.when(step == 0)
    def _():
        qd = keep(scale * mm(dy[...], bd[...], 1, 1), ids[...], rank)
        qd_s[...] = qd
        qdt_s[...] = qd.T
        acc[...] = jnp.zeros_like(acc)
        qg_acc[...] = jnp.zeros_like(qg_acc)
        qu_acc[...] = jnp.zeros_like(qu_acc)

    gate, up = gate_r[...], up_r[...]
    sig = jax.nn.sigmoid(gate)
    act = gate * sig
    gad_o[...] = mm(qdt_s[...], (act * up).astype(bf))
    dh = mm(dy[...], wd[...], 1, 1) + rounded(mm(qd_s[...], ad[...]))
    dg = (dh * up * sig * (1.0 + gate * (1.0 - sig))).astype(bf)
    du = (dh * act).astype(bf)
    dg_o[...] = dg
    du_o[...] = du
    acc[...] += mm(dg, wg[...], 1, 1) + mm(du, wu[...], 1, 1)
    qg_acc[...] += mm(dg, bg[...], 1, 1)
    qu_acc[...] += mm(du, bu[...], 1, 1)

    @pl.when(step == pl.num_programs(0) - 1)
    def _():
        qg = keep(scale * qg_acc[...], ids[...], rank)
        qu = keep(scale * qu_acc[...], ids[...], rank)
        qg_o[...] = qg
        qu_o[...] = qu
        lora = rounded(mm(qg, ag[...]) + mm(qu, au[...]))
        dx_o[...] = (dy[...].astype(f32) + acc[...] + lora).astype(bf)


def grads_body(scale, wide, pg, pu, pd, qg, qu, x, dy, dg, du, gbg, gbu, gag, gau, gbd, pgt, put, pdt, qgt, qut):
    step = pl.program_id(0)

    @pl.when(step == 0)
    def _():
        for src, dst in ((pg, pgt), (pu, put), (pd, pdt), (qg, qgt), (qu, qut)):
            dst[...] = src[...].T

    @pl.when(step < wide)
    def _():
        gbg[...] = scale * mm(pgt[...], dg[...])
        gbu[...] = scale * mm(put[...], du[...])

    @pl.when(step >= wide)
    def _():
        gag[...] = mm(qgt[...], x[...])
        gau[...] = mm(qut[...], x[...])
        gbd[...] = scale * mm(pdt[...], dy[...])


def whole(shape):
    return pl.BlockSpec(shape, lambda j: (0, 0), pipeline_mode=pl.Buffered(1))


def kept(shape):
    return pl.BlockSpec(shape, lambda j: (0, 0))


def cols(rows):
    return pl.BlockSpec((rows, TILE), lambda j: (0, j))


def params():
    return pltpu.CompilerParams(dimension_semantics=('arbitrary',), vmem_limit_bytes=60 * 2 ** 20)


def cost(flops, nbytes):
    return pl.CostEstimate(flops=flops, bytes_accessed=nbytes, transcendentals=0)


def solution(mesh):
    group = mesh.shape['data']
    tok_spec = P(('rep', 'data'), None)
    id_spec = P(('rep', 'data'))
    full_spec = P(None, None)
    own_spec = P('data', None, None)
    grad_spec = P(('rep', 'data'), None, None)

    def device_fn(x_loc, ids_loc, dy_loc, w_gate, w_up, w_down, a_gate, b_gate, a_up, b_up, a_down, b_down):
        tokens, dim = x_loc.shape
        n_local, _, rank = a_gate.shape
        hidden = w_gate.shape[1]
        width = n_local * rank
        scale = LORA_ALPHA / rank
        cap = ((3 * tokens + 8 * group - 1) // (8 * group)) * 8
        rows = group * cap
        steps = hidden // TILE
        owner = ids_loc // n_local
        local = ids_loc % n_local
        before = (owner[:, None] == owner[None, :]) & (jnp.arange(tokens)[None, :] < jnp.arange(tokens)[:, None])
        slot = owner * cap + before.astype(jnp.int32).sum(axis=1)
        hit = jnp.arange(rows)[:, None] == slot[None, :]
        pack = hit.astype(bf)
        slot_ids = jnp.where(hit, local[None, :] + 1, 0).max(axis=1) - 1

        def exchange(arr):
            return lax.all_to_all(arr, 'data', 0, 0, tiled=True)

        ids = exchange(slot_ids)[:, None]
        x = exchange(mm(pack, x_loc).astype(bf))
        dy = exchange(mm(pack, dy_loc).astype(bf))

        def as_rows(weight):
            return jnp.swapaxes(weight, 1, 2).reshape(width, weight.shape[1])

        ag, au, ad = as_rows(a_gate), as_rows(a_up), as_rows(a_down)
        bg, bu, bd = b_gate.reshape(width, hidden), b_up.reshape(width, hidden), b_down.reshape(width, dim)

        def arr(shape, dtype):
            return jax.ShapeDtypeStruct(shape, dtype)

        base = 2 * rows * dim * hidden
        lora = 2 * rows * width * hidden
        small = 2 * rows * width * dim
        shared = [whole((rows, 1)), whole((rows, dim)), whole((width, dim)), whole((width, dim)), whole((width, dim))]
        weights = [cols(dim), cols(dim), pl.BlockSpec((TILE, dim), lambda j: (j, 0)), cols(width), cols(width), cols(width)]
        gate, up, out, pg, pu, pd = pl.pallas_call(
            functools.partial(forward_body, rank, scale),
            grid=(steps,),
            in_specs=shared + weights,
            out_specs=[cols(rows), cols(rows), kept((rows, dim))] + [kept((rows, width))] * 3,
            out_shape=[arr((rows, hidden), f32)] * 2 + [arr((rows, dim), bf)] + [arr((rows, width), bf)] * 3,
            scratch_shapes=[pltpu.VMEM((rows, dim), f32), pltpu.VMEM((rows, width), f32)],
            compiler_params=params(),
            cost_estimate=cost(3 * base + 3 * lora + 3 * small, 6 * dim * hidden + 8 * rows * hidden),
            name='forward',
        )(ids, x, ag, au, bd, w_gate, w_up, w_down, bg, bu, ad)
        dg, du, g_ad, dx, qg, qu = pl.pallas_call(
            functools.partial(backward_body, rank, scale),
            grid=(steps,),
            in_specs=shared + [cols(rows), cols(rows)] + weights,
            out_specs=[cols(rows), cols(rows), cols(width), kept((rows, dim)), kept((rows, width)), kept((rows, width))],
            out_shape=[arr((rows, hidden), bf)] * 2 + [arr((width, hidden), f32), arr((rows, dim), bf)] + [arr((rows, width), bf)] * 2,
            scratch_shapes=[pltpu.VMEM((rows, dim), f32), pltpu.VMEM((rows, width), f32), pltpu.VMEM((rows, width), f32),
                            pltpu.VMEM((rows, width), bf), pltpu.VMEM((width, rows), bf)],
            compiler_params=params(),
            cost_estimate=cost(3 * base + 4 * lora + 3 * small, 6 * dim * hidden + 8 * rows * hidden),
            name='backward',
        )(ids, dy, ag, au, bd, gate, up, w_gate, w_up, w_down, bg, bu, ad)
        wide_cols = pl.BlockSpec((rows, TILE), lambda j: (0, jnp.minimum(j, steps - 1)))
        wide_grad = pl.BlockSpec((width, TILE), lambda j: (0, jnp.minimum(j, steps - 1)))
        slim_cols = pl.BlockSpec((rows, TILE), lambda j: (0, jnp.maximum(j - steps, 0)))
        slim_grad = pl.BlockSpec((width, TILE), lambda j: (0, jnp.maximum(j - steps, 0)))
        g_bg, g_bu, g_ag, g_au, g_bd = pl.pallas_call(
            functools.partial(grads_body, scale, steps),
            grid=(steps + dim // TILE,),
            in_specs=[whole((rows, width))] * 5 + [slim_cols, slim_cols, wide_cols, wide_cols],
            out_specs=[wide_grad, wide_grad, slim_grad, slim_grad, slim_grad],
            out_shape=[arr((width, hidden), f32)] * 2 + [arr((width, dim), f32)] * 3,
            scratch_shapes=[pltpu.VMEM((width, rows), bf)] * 5,
            compiler_params=params(),
            cost_estimate=cost(2 * lora + 3 * small, 8 * width * hidden),
            name='adapter_grads',
        )(pg, pu, pd, qg, qu, x, dy, dg, du)

        def back(vals):
            return mm(pack, exchange(vals), 0, 0).astype(bf)

        def a_grad(vals):
            return jnp.swapaxes(vals.reshape(n_local, rank, vals.shape[1]), 1, 2)

        def b_grad(vals):
            return vals.reshape(n_local, rank, vals.shape[1])

        return back(out), back(dx), a_grad(g_ag), b_grad(g_bg), a_grad(g_au), b_grad(g_bu), a_grad(g_ad), b_grad(g_bd)

    return jax.shard_map(
        device_fn,
        mesh=mesh,
        in_specs=(tok_spec, id_spec, tok_spec, full_spec, full_spec, full_spec) + (own_spec,) * 6,
        out_specs=(tok_spec, tok_spec) + (grad_spec,) * 6,
        check_vma=False,
    )
```

profile of v0, /device:TPU:0, one launch (start us, length us, event | category | flops | bytes accessed | tf_op | source)
XLA Modules:
  0.0 224.2 jit_solution(12246922136813215332)
XLA Ops:
  0.6 0.0 copy-start
  0.6 0.7 and_select_fusion.1
  1.4 0.2 convert_reduce_fusion
  1.6 0.2 select_reduce_fusion
  1.7 0.7 sub.14
  2.4 4.3 %all-to-all-start = ((s32[8,48,1]{1,2,0:T(1,128)}), s32[8,48,1]{1,2,0:T(1,128)S(1)}, u32[]{:S(2)}, u32[]{:S(2)}) async-start(s32[8,48,1]{1,2,0:T(1,128)} %sub.14), calls=%async_computation | async-start | bytes 8192 | tf_op jit(solution)/shard_map/all_to_all | solution.py:156
  6.7 1.7 convolution_convert_fusion.1
  8.4 2.8 %all-to-all-done = s32[8,48,1]{1,2,0:T(1,128)S(1)} async-done(((s32[8,48,1]{1,2,0:T(1,128)}), s32[8,48,1]{1,2,0:T(1,128)S(1)}, u32[]{:S(2)}, u32[]{:S(2)}) %all-to-all-start) | async-done | bytes 1568 | tf_op jit(solution)/shard_map/all_to_all | solution.py:156
  11.2 2.3 %all-to-all-start.1 = ((bf16[8,48,2048]{2,1,0:T(8,128)(2,1)}), bf16[8,48,2048]{2,1,0:T(8,128)(2,1)S(1)}, u32[]{:S(2)}, u32[]{:S(2)}) async-start(bf16[8,48,2048]{2,1,0:T(8,128)(2,1)} %bitcast), calls=%async_computation.1 | async-start | bytes 3145728 | tf_op jit(solution)/shard_map/all_to_all | solution.py:156
  13.6 1.7 convolution_convert_fusion
  15.3 0.5 broadcast.50
  15.8 0.7 reduce.3
  16.4 0.8 broadcast_in_dim.25.ids
  17.2 17.2 %all-to-all-done.1 = bf16[8,48,2048]{2,1,0:T(8,128)(2,1)S(1)} async-done(((bf16[8,48,2048]{2,1,0:T(8,128)(2,1)}), bf16[8,48,2048]{2,1,0:T(8,128)(2,1)S(1)}, u32[]{:S(2)}, u32[]{:S(2)}) %all-to-all-start.1) | async-done | bytes 1572896 | tf_op jit(solution)/shard_map/all_to_all | solution.py:156
  34.5 2.3 %all-to-all-start.3 = ((bf16[8,48,2048]{2,1,0:T(8,128)(2,1)}), bf16[8,48,2048]{2,1,0:T(8,128)(2,1)S(1)}, u32[]{:S(2)}, u32[]{:S(2)}) async-start(bf16[8,48,2048]{2,1,0:T(8,128)(2,1)} %bitcast.13), calls=%async_computation.3 | async-start | bytes 3145728 | tf_op jit(solution)/shard_map/all_to_all | solution.py:156
  36.8 68.6 %forward.1 = (f32[384,8192]{1,0:T(8,128)}, f32[384,8192]{1,0:T(8,128)}, bf16[384,2048]{1,0:T(8,128)(2,1)}, bf16[384,512]{1,0:T(8,128)(2,1)}, bf16[384,512]{1,0:T(8,128)(2,1)}, /*index=5*/bf16[384,512]{1,0:T(8,128)(2,1)}) custom-call(s32[384,1]{1,0:T(8,128)} %broadcast_in_dim.25.ids, bf16[384,2048]{1,0:T(8,128)(2,1)} %bitcast.38, bf16[512,2048]{1,0:T(8,128)(2,1)} %bitcast.50, ...), custom_call_target="tpu_custom_call" | custom-call | flops 50734301184 | bytes 125829120 | tf_op jit(solution)/shard_map/forward/pallas_call | solution.py:176
  105.4 0.0 all-to-all-done.3
  105.4 1.1 copy-done.3
  106.6 2.9 %all-to-all-start.2 = ((bf16[8,48,2048]{2,1,0:T(8,128)(2,1)}), bf16[8,48,2048]{2,1,0:T(8,128)(2,1)S(1)}, u32[]{:S(2)}, u32[]{:S(2)}) async-start(bf16[8,48,2048]{2,1,0:T(8,128)(2,1)} %bitcast.43), calls=%async_computation.2 | async-start | bytes 3145728 | tf_op jit(solution)/shard_map/all_to_all | solution.py:156
  109.4 77.8 %backward.1 = (bf16[384,8192]{1,0:T(8,128)(2,1)}, bf16[384,8192]{1,0:T(8,128)(2,1)}, f32[512,8192]{1,0:T(8,128)}, bf16[384,2048]{1,0:T(8,128)(2,1)}, bf16[384,512]{1,0:T(8,128)(2,1)}, /*index=5*/bf16[384,512]{1,0:T(8,128)(2,1)}) custom-call(s32[384,1]{1,0:T(8,128)} %broadcast_in_dim.25.ids, bf16[384,2048]{1,0:T(8,128)(2,1)} %bitcast.40, ...), custom_call_target="tpu_custom_call" | custom-call | flops 53955526656 | bytes 125829120 | tf_op jit(solution)/shard_map/backward/pallas_call | solution.py:187
  187.3 3.1 %all-to-all-start.4 = ((bf16[8,48,2048]{2,1,0:T(8,128)(2,1)}), bf16[8,48,2048]{2,1,0:T(8,128)(2,1)}, u32[]{:S(2)}, u32[]{:S(2)}) async-start(bf16[8,48,2048]{2,1,0:T(8,128)(2,1)} %bitcast.42), calls=%async_computation.4 | async-start | bytes 3145728 | tf_op jit(solution)/shard_map/all_to_all | solution.py:156
  190.3 29.9 %adapter_grads.1 = (f32[512,8192]{1,0:T(8,128)}, f32[512,8192]{1,0:T(8,128)}, f32[512,2048]{1,0:T(8,128)}, f32[512,2048]{1,0:T(8,128)}, f32[512,2048]{1,0:T(8,128)}) custom-call(bf16[384,512]{1,0:T(8,128)(2,1)} %get-tuple-element.29.pg, bf16[384,512]{1,0:T(8,128)(2,1)} %get-tuple-element.30.pu, bf16[384,512]{1,0:T(8,128)(2,1)} %get-tuple-element.31.pd, ...), custom_call_target="tpu_custom_call" | custom-call | flops 8858370048 | bytes 33554432 | tf_op jit(solution)/shard_map/adapter_grads/pallas_call | solution.py:203
  220.2 1.3 convolution_convert_fusion.3
  221.5 2.7 %convolution_convert_fusion.2 = bf16[128,2048]{1,0:T(8,128)(2,1)} fusion(bf16[384,2048]{1,0:T(8,128)(2,1)} %bitcast.19, s32[128]{0:T(128)S(1)} %multiply_add_fusion), kind=kOutput, calls=%fused_computation.2 | convolution fusion | flops 201637888 | bytes 2097664 | tf_op jit(solution)/shard_map/dot_general | solution.py:17
  (12 shorter events, 0.0 us)
Async XLA Ops:
  0.6 6.1 %copy-start = (bf16[128,2048]{1,0:T(8,128)(2,1)S(1)}, bf16[128,2048]{1,0:T(8,128)(2,1)}, u32[]{:S(2)}) copy-start(bf16[128,2048]{1,0:T(8,128)(2,1)} %param.12) | copy-start | bytes 1572868
  2.4 8.8 %all-to-all-start = ((s32[8,48,1]{1,2,0:T(1,128)}), s32[8,48,1]{1,2,0:T(1,128)S(1)}, u32[]{:S(2)}, u32[]{:S(2)}) async-start(s32[8,48,1]{1,2,0:T(1,128)} %sub.14), calls=%async_computation | async-start | bytes 8192 | tf_op jit(solution)/shard_map/all_to_all | solution.py:156
  8.4 5.1 %copy-start.4 = (bf16[128,2048]{1,0:T(8,128)(2,1)S(1)}, bf16[128,2048]{1,0:T(8,128)(2,1)}, u32[]{:S(2)}) copy-start(bf16[128,2048]{1,0:T(8,128)(2,1)} %param.14) | copy-start | bytes 1572868
  11.2 23.2 %all-to-all-start.1 = ((bf16[8,48,2048]{2,1,0:T(8,128)(2,1)}), bf16[8,48,2048]{2,1,0:T(8,128)(2,1)S(1)}, u32[]{:S(2)}, u32[]{:S(2)}) async-start(bf16[8,48,2048]{2,1,0:T(8,128)(2,1)} %bitcast), calls=%async_computation.1 | async-start | bytes 3145728 | tf_op jit(solution)/shard_map/all_to_all | solution.py:156
  34.5 2.3 %copy-start.2 = (bf16[8,48,2048]{2,1,0:T(8,128)(2,1)}, bf16[8,48,2048]{2,1,0:T(8,128)(2,1)S(1)}, u32[]{:S(2)}) copy-start(bf16[8,48,2048]{2,1,0:T(8,128)(2,1)S(1)} %all-to-all-done.1) | copy-start | bytes 4718596
  34.5 71.0 %all-to-all-start.3 = ((bf16[8,48,2048]{2,1,0:T(8,128)(2,1)}), bf16[8,48,2048]{2,1,0:T(8,128)(2,1)S(1)}, u32[]{:S(2)}, u32[]{:S(2)}) async-start(bf16[8,48,2048]{2,1,0:T(8,128)(2,1)} %bitcast.13), calls=%async_computation.3 | async-start | bytes 3145728 | tf_op jit(solution)/shard_map/all_to_all | solution.py:156
  105.4 1.1 copy-start.3
  106.6 80.7 %all-to-all-start.2 = ((bf16[8,48,2048]{2,1,0:T(8,128)(2,1)}), bf16[8,48,2048]{2,1,0:T(8,128)(2,1)S(1)}, u32[]{:S(2)}, u32[]{:S(2)}) async-start(bf16[8,48,2048]{2,1,0:T(8,128)(2,1)} %bitcast.43), calls=%async_computation.2 | async-start | bytes 3145728 | tf_op jit(solution)/shard_map/all_to_all | solution.py:156
  187.3 34.2 %all-to-all-start.4 = ((bf16[8,48,2048]{2,1,0:T(8,128)(2,1)}), bf16[8,48,2048]{2,1,0:T(8,128)(2,1)}, u32[]{:S(2)}, u32[]{:S(2)}) async-start(bf16[8,48,2048]{2,1,0:T(8,128)(2,1)} %bitcast.42), calls=%async_computation.4 | async-start | bytes 3145728 | tf_op jit(solution)/shard_map/all_to_all | solution.py:156
  220.2 4.0 %copy-start.1 = (bf16[128,2048]{1,0:T(8,128)(2,1)S(1)}, bf16[128,2048]{1,0:T(8,128)(2,1)}, u32[]{:S(2)}) copy-start(bf16[128,2048]{1,0:T(8,128)(2,1)} %param.12) | copy-start | bytes 1572868
where the time goes:
time: 225 us; the launch traced here: 224 us
  Pallas kernels  176 us (78%)
  waiting for transfers between devices  20 us (9%)
  starting transfers between devices  14.9 us (7%)
  matrix products  7.39 us (3%)
  local copies, waits for them, and re-layouts  3.15 us (1%)
    pallas_call x1, Pallas kernels, device_fn(): pl.pallas_call(functools.partial(backward_body, rank, scale), grid=(steps...  77.8 us
    pallas_call x1, Pallas kernels, device_fn(): pl.pallas_call(functools.partial(forward_body, rank, scale), grid=(steps,...  68.6 us
    pallas_call x1, Pallas kernels, device_fn(): pl.pallas_call(functools.partial(grads_body, scale, steps), grid=(steps +...  29.9 us
    all_to_all x5, waiting for transfers between devices, exchange(): return lax.all_to_all(arr, 'data', 0, 0, tiled=True)  20 us
    all_to_all x5, starting transfers between devices, exchange(): return lax.all_to_all(arr, 'data', 0, 0, tiled=True)  14.9 us
    dot_general x4, matrix products, mm(): lax.dot_general(left, right, (((ldim,), (rdim,)), ((), ())), preferred_el...  7.39 us
  transfers between devices with their start and end apart: 5, of which 2 were waited for; matrix products, arithmetic and copies ran while one was open for 3% of the time, Pallas kernels for 79%

commit v1 on v0

--- a/solution.py
+++ b/solution.py
@@ -26,29 +26,208 @@
     return jnp.where(cols == ids, vals, 0.0).astype(bf)
 
 
-def forward_body(rank, scale, ids, x, ag, au, bd, wg, wu, wd, bg, bu, ad, gate_o, up_o, out_o, pg_o, pu_o, pd_o, acc, pd_acc):
-    step = pl.program_id(0)
-
-    @pl.when(step == 0)
-    def _():
-        pg_o[...] = keep(mm(x[...], ag[...], 1, 1), ids[...], rank)
-        pu_o[...] = keep(mm(x[...], au[...], 1, 1), ids[...], rank)
-        acc[...] = jnp.zeros_like(acc)
-        pd_acc[...] = jnp.zeros_like(pd_acc)
-
-    gate = mm(x[...], wg[...]) + rounded(scale * mm(pg_o[...], bg[...]))
-    up = mm(x[...], wu[...]) + rounded(scale * mm(pu_o[...], bu[...]))
-    gate_o[...] = gate
-    up_o[...] = up
-    h = (gate * jax.nn.sigmoid(gate) * up).astype(bf)
-    acc[...] += mm(h, wd[...])
-    pd_acc[...] += mm(h, ad[...], 1, 1)
-
-    @pl.when(step == pl.num_programs(0) - 1)
-    def _():
-        pd = keep(pd_acc[...], ids[...], rank)
-        pd_o[...] = pd
-        out_o[...] = (x[...].astype(f32) + acc[...] + rounded(scale * mm(pd, bd[...]))).astype(bf)
+def forward_body(cap, n_local, rank, scale, axes, ids_r, x_loc, dy_loc, ag_h, au_h, bd_h, wg, wu, wd, bg, bu, ad,
+                 x_o, dy_o, gate_o, up_o, out_o, ids_o, pg_o, pu_o, pd_o,
+                 gu, x_own, dy_own, xs, dys, ids_s, ids_v, wbuf, bbuf, small, acc, pd_acc,
+                 send_sem, recv_sem, wsem, bsem, ssem, gsem, osem):
+    group, dim = ids_s.shape[0], x_loc.shape[1]
+    tokens, hidden = x_loc.shape[0], wg.shape[1]
+    rows = group * cap
+    part = wbuf.shape[1]
+    n_slots = wbuf.shape[0]
+    chunks = dim // part
+    across = hidden // dim
+    first = chunks * 2 * across
+    steps = hidden // part
+    rep, me = lax.axis_index(axes[0]), lax.axis_index(axes[1])
+
+    def peer(k):
+        return lax.rem(me + k, group)
+
+    barrier = pltpu.get_barrier_semaphore()
+    for k in range(1, group):
+        pl.semaphore_signal(barrier, inc=1, device_id=(rep, peer(k)), device_id_type=pl.DeviceIdType.MESH)
+
+    def tile_copy(src, slot):
+        return pltpu.make_async_copy(src, wbuf.at[slot], wsem.at[slot])
+
+    def start_tile(t):
+        slot = lax.rem(t, n_slots)
+        which = lax.rem(lax.div(t, across), 2)
+        src = (pl.ds(pl.multiple_of(lax.div(t, 2 * across) * part, part), part),
+               pl.ds(pl.multiple_of(lax.rem(t, across) * dim, dim), dim))
+
+        @pl.when((t < first) & (which == 0))
+        def _():
+            tile_copy(wg.at[src], slot).start()
+
+        @pl.when((t < first) & (which == 1))
+        def _():
+            tile_copy(wu.at[src], slot).start()
+
+        @pl.when((t >= first) & (t < first + steps))
+        def _():
+            tile_copy(wd.at[pl.ds(pl.multiple_of((t - first) * part, part), part)], slot).start()
+
+    def wait_tile(t):
+        slot = lax.rem(t, n_slots)
+        tile_copy(wd.at[pl.ds(0, part)], slot).wait()
+        return slot
+
+    def adapter_copies(j, slot):
+        span = pl.ds(pl.multiple_of(j * part, part), part)
+        return [pltpu.make_async_copy(src.at[:, span], bbuf.at[slot, i], bsem.at[slot, i]) for i, src in enumerate((bg, bu, ad))]
+
+    small_copies = [pltpu.make_async_copy(src, small.at[i], ssem.at[i]) for i, src in enumerate((ag_h, au_h, bd_h))]
+
+    def fill(t, carry):
+        start_tile(t)
+        return carry
+
+    lax.fori_loop(0, n_slots, fill, 0)
+    for copy in small_copies:
+        copy.start()
+    for j in range(2):
+        for copy in adapter_copies(j, j):
+            copy.start()
+
+    ids = ids_r[...]
+    owner = lax.div(ids, jnp.int32(n_local))
+    local = lax.rem(ids, jnp.int32(n_local))
+    owner_to = jnp.broadcast_to(owner.astype(f32), (tokens, tokens))
+    earlier = lax.broadcasted_iota(jnp.int32, (tokens, tokens), 0) < lax.broadcasted_iota(jnp.int32, (tokens, tokens), 1)
+    rank_in = jnp.sum(jnp.where((owner_to.T == owner_to) & earlier, 1.0, 0.0), axis=0, keepdims=True).astype(jnp.int32)
+    pack = jnp.where(lax.broadcasted_iota(jnp.int32, (rows, tokens), 0) == owner * cap + rank_in, 1.0, 0.0).astype(bf)
+    lanes = 128
+    spread = jnp.where(lax.broadcasted_iota(jnp.int32, (group * lanes, tokens), 0) == owner * lanes + rank_in, 1.0, 0.0).astype(bf)
+    tagged = mm(jnp.broadcast_to((local + 1).astype(f32), (8, tokens)).astype(bf), spread, 1, 1)
+    for d in range(group):
+        ids_s[d] = tagged[:, d * lanes:(d + 1) * lanes]
+
+    def pack_part(src, dst, c):
+        span = slice(c * part, (c + 1) * part)
+        dst[:, span] = mm(pack, src[:, span]).astype(bf)
+
+    mine = pl.ds(pl.multiple_of(me * cap, 16), cap)
+
+    def row_copy(src, dst, span, c, k):
+        there = pl.ds(pl.multiple_of(peer(k) * cap, 16), cap)
+        return pltpu.make_async_remote_copy(
+            src_ref=src.at[there, span], dst_ref=dst.at[mine, span], send_sem=send_sem.at[c, k], recv_sem=recv_sem.at[c, k],
+            device_id=(rep, peer(k)), device_id_type=pl.DeviceIdType.MESH)
+
+    def id_copy(k):
+        return pltpu.make_async_remote_copy(
+            src_ref=ids_s.at[peer(k)], dst_ref=ids_v.at[me], send_sem=send_sem.at[chunks + 1, k], recv_sem=recv_sem.at[chunks + 1, k],
+            device_id=(rep, peer(k)), device_id_type=pl.DeviceIdType.MESH)
+
+    x_copies = [[row_copy(xs, x_own, pl.ds(c * part, part), c, k) for k in range(1, group)] for c in range(chunks)]
+    dy_copies = [row_copy(dys, dy_own, pl.ds(0, dim), chunks, k) for k in range(1, group)]
+    id_copies = [id_copy(k) for k in range(1, group)]
+
+    pack_part(x_loc, xs, 0)
+    pl.semaphore_wait(barrier, group - 1)
+    for c in range(chunks):
+        if c + 1 < chunks:
+            pack_part(x_loc, xs, c + 1)
+        for copy in x_copies[c]:
+            copy.start()
+    for copy in id_copies:
+        copy.start()
+    for c in range(chunks):
+        pack_part(dy_loc, dys, c)
+    x_own[mine, :] = xs[mine, :]
+    dy_own[mine, :] = dys[mine, :]
+    ids_v[me] = ids_s[me]
+    for copy in dy_copies:
+        copy.start()
+
+    def clear(i, carry):
+        gu[0, pl.ds(pl.multiple_of(i * 8, 8), 8), :] = jnp.zeros((8, hidden), f32)
+        gu[1, pl.ds(pl.multiple_of(i * 8, 8), 8), :] = jnp.zeros((8, hidden), f32)
+        return carry
+
+    lax.fori_loop(0, rows // 8, clear, 0)
+    acc[...] = jnp.zeros_like(acc)
+    pd_acc[...] = jnp.zeros_like(pd_acc)
+
+    for c in range(chunks):
+        for copy in x_copies[c]:
+            copy.wait_recv()
+
+        def pre_step(i, carry):
+            t = c * 2 * across + i
+            slot = wait_tile(t)
+            span = pl.ds(pl.multiple_of(lax.rem(i, across) * dim, dim), dim)
+            which = lax.div(i, across)
+            gu[which, :, span] += mm(x_own[:, c * part:(c + 1) * part], wbuf[slot])
+            start_tile(t + n_slots)
+            return carry
+
+        lax.fori_loop(0, 2 * across, pre_step, 0)
+
+    for copy in id_copies:
+        copy.wait_recv()
+    got = jnp.concatenate([ids_v[s, 0:1, :] for s in range(group)] + [jnp.zeros((lanes - group, lanes), f32)], axis=0).T
+    ids_col = jnp.concatenate([got[0:cap, s:s + 1] for s in range(group)], axis=0).astype(jnp.int32) - 1
+    ids_o[...] = ids_col
+    x_out = pltpu.make_async_copy(x_own, x_o, osem.at[0])
+    x_out.start()
+    for copy in small_copies[:2]:
+        copy.wait()
+    pg_o[...] = keep(mm(x_own[...], small[0], 1, 1), ids_col, rank)
+    pu_o[...] = keep(mm(x_own[...], small[1], 1, 1), ids_col, rank)
+
+    def gu_copies(j):
+        span = pl.ds(pl.multiple_of(j * part, part), part)
+        return [pltpu.make_async_copy(gu.at[i, :, span], dst.at[:, span], gsem.at[j, i]) for i, dst in enumerate((gate_o, up_o))]
+
+    def step(j, carry):
+        t = first + j
+        span = pl.ds(pl.multiple_of(j * part, part), part)
+        two = lax.rem(j, 2)
+        for copy in adapter_copies(0, two):
+            copy.wait()
+        gate = gu[0, :, span] + rounded(scale * mm(pg_o[...], bbuf[two, 0]))
+        up = gu[1, :, span] + rounded(scale * mm(pu_o[...], bbuf[two, 1]))
+        gu[0, :, span] = gate
+        gu[1, :, span] = up
+        h = (gate * jax.nn.sigmoid(gate) * up).astype(bf)
+        slot = wait_tile(t)
+        acc[...] += mm(h, wbuf[slot])
+        pd_acc[...] += mm(h, bbuf[two, 2], 1, 1)
+        for copy in gu_copies(j):
+            copy.start()
+        start_tile(t + n_slots)
+
+        @pl.when(j + 2 < steps)
+        def _():
+            for copy in adapter_copies(j + 2, two):
+                copy.start()
+
+        return carry
+
+    lax.fori_loop(0, steps, step, 0)
+    for copy in dy_copies:
+        copy.wait_recv()
+    dy_out = pltpu.make_async_copy(dy_own, dy_o, osem.at[1])
+    dy_out.start()
+    small_copies[2].wait()
+    pd = keep(pd_acc[...], ids_col, rank)
+    pd_o[...] = pd
+    out_o[...] = (x_own[...].astype(f32) + acc[...] + rounded(scale * mm(pd, small[2]))).astype(bf)
+
+    def drain(j, carry):
+        for copy in gu_copies(j):
+            copy.wait()
+        return carry
+
+    lax.fori_loop(0, steps, drain, 0)
+    for copies in x_copies + [dy_copies, id_copies]:
+        for copy in copies:
+            copy.wait_send()
+    x_out.wait()
+    dy_out.wait()
 
 
 def backward_body(rank, scale, ids, dy, ag, au, bd, gate_r, up_r, wg, wu, wd, bg, bu, ad,
@@ -144,20 +323,9 @@
         cap = ((3 * tokens + 8 * group - 1) // (8 * group)) * 8
         rows = group * cap
         steps = hidden // TILE
-        owner = ids_loc // n_local
-        local = ids_loc % n_local
-        before = (owner[:, None] == owner[None, :]) & (jnp.arange(tokens)[None, :] < jnp.arange(tokens)[:, None])
-        slot = owner * cap + before.astype(jnp.int32).sum(axis=1)
-        hit = jnp.arange(rows)[:, None] == slot[None, :]
-        pack = hit.astype(bf)
-        slot_ids = jnp.where(hit, local[None, :] + 1, 0).max(axis=1) - 1
 
         def exchange(arr):
             return lax.all_to_all(arr, 'data', 0, 0, tiled=True)
-
-        ids = exchange(slot_ids)[:, None]
-        x = exchange(mm(pack, x_loc).astype(bf))
-        dy = exchange(mm(pack, dy_loc).astype(bf))
 
         def as_rows(weight):
             return jnp.swapaxes(weight, 1, 2).reshape(width, weight.shape[1])
@@ -173,17 +341,28 @@
         small = 2 * rows * width * dim
         shared = [whole((rows, 1)), whole((rows, dim)), whole((width, dim)), whole((width, dim)), whole((width, dim))]
         weights = [cols(dim), cols(dim), pl.BlockSpec((TILE, dim), lambda j: (j, 0)), cols(width), cols(width), cols(width)]
-        gate, up, out, pg, pu, pd = pl.pallas_call(
-            functools.partial(forward_body, rank, scale),
-            grid=(steps,),
-            in_specs=shared + weights,
-            out_specs=[cols(rows), cols(rows), kept((rows, dim))] + [kept((rows, width))] * 3,
-            out_shape=[arr((rows, hidden), f32)] * 2 + [arr((rows, dim), bf)] + [arr((rows, width), bf)] * 3,
-            scratch_shapes=[pltpu.VMEM((rows, dim), f32), pltpu.VMEM((rows, width), f32)],
-            compiler_params=params(),
+        chunks = dim // TILE
+        any_spec = pl.BlockSpec(memory_space=pl.ANY)
+        vmem_spec = pl.BlockSpec(memory_space=pltpu.VMEM)
+        sem = pltpu.SemaphoreType.DMA
+        x, dy, gate, up, out, ids, pg, pu, pd = pl.pallas_call(
+            functools.partial(forward_body, cap, n_local, rank, scale, mesh.axis_names),
+            in_specs=[vmem_spec] * 3 + [any_spec] * 9,
+            out_specs=[any_spec] * 4 + [vmem_spec] * 5,
+            out_shape=[arr((rows, dim), bf)] * 2 + [arr((rows, hidden), f32)] * 2 + [arr((rows, dim), bf), arr((rows, 1), jnp.int32)]
+            + [arr((rows, width), bf)] * 3,
+            scratch_shapes=[
+                pltpu.VMEM((2, rows, hidden), f32),
+                pltpu.VMEM((rows, dim), bf), pltpu.VMEM((rows, dim), bf), pltpu.VMEM((rows, dim), bf), pltpu.VMEM((rows, dim), bf),
+                pltpu.VMEM((group, 8, 128), f32), pltpu.VMEM((group, 8, 128), f32),
+                pltpu.VMEM((4, TILE, dim), bf), pltpu.VMEM((2, 3, width, TILE), bf), pltpu.VMEM((3, width, dim), bf),
+                pltpu.VMEM((rows, dim), f32), pltpu.VMEM((rows, width), f32),
+                sem((chunks + 2, group)), sem((chunks + 2, group)), sem((4,)), sem((2, 3)), sem((3,)), sem((steps, 2)), sem((2,)),
+            ],
+            compiler_params=pltpu.CompilerParams(collective_id=0, has_side_effects=True, vmem_limit_bytes=63 * 2 ** 20),
             cost_estimate=cost(3 * base + 3 * lora + 3 * small, 6 * dim * hidden + 8 * rows * hidden),
             name='forward',
-        )(ids, x, ag, au, bd, w_gate, w_up, w_down, bg, bu, ad)
+        )(ids_loc[None, :], x_loc, dy_loc, ag, au, bd, w_gate, w_up, w_down, bg, bu, ad)
         dg, du, g_ad, dx, qg, qu = pl.pallas_call(
             functools.partial(backward_body, rank, scale),
             grid=(steps,),
@@ -212,6 +391,11 @@
             name='adapter_grads',
         )(pg, pu, pd, qg, qu, x, dy, dg, du)
 
+        owner = ids_loc // n_local
+        before = (owner[:, None] == owner[None, :]) & (jnp.arange(tokens)[None, :] < jnp.arange(tokens)[:, None])
+        slot = owner * cap + before.astype(jnp.int32).sum(axis=1)
+        pack = (jnp.arange(rows)[:, None] == slot[None, :]).astype(bf)
+
         def back(vals):
             return mm(pack, exchange(vals), 0, 0).astype(bf)
 

time: 225 us -> 200 us (0.89)
  waiting for transfers between devices: 20 us -> 0.01 us
  Pallas kernels: 176 us -> 190 us
  starting transfers between devices: 14.9 us -> 5.99 us
  matrix products: 7.39 us -> 2.57 us
  local copies, waits for them, and re-layouts: 3.15 us -> 0.01 us
    all_to_all x5 -> x2, waiting for transfers between devices: 20 us -> 0.01 us  [exchange(): return lax.all_to_all(arr, 'data', 0, 0, tiled=True)]
    pallas_call x1, Pallas kernels: 68.6 us -> 82.2 us  [device_fn(): pl.pallas_call(functools.partial(forward_body, cap, n_local, rank, scale,...]
    all_to_all x5 -> x2, starting transfers between devices: 14.9 us -> 5.99 us  [exchange(): return lax.all_to_all(arr, 'data', 0, 0, tiled=True)]
    dot_general x4 -> x2, matrix products: 7.39 us -> 2.57 us  [mm(): lax.dot_general(left, right, (((ldim,), (rdim,)), ((), ())), preferred_el...]
  transfers between devices with their start and end apart: 5 -> 2, of which waited for: 2 -> 0; matrix products, arithmetic and copies ran while one was open for 3% -> 1% of each run, Pallas kernels for 79% -> 54%
where the time goes in v1:
time: 200 us; the launch traced here: 199 us
  Pallas kernels  190 us (95%)
  starting transfers between devices  5.99 us (3%)
  matrix products  2.57 us (1%)
    pallas_call x1, Pallas kernels, device_fn(): pl.pallas_call(functools.partial(forward_body, cap, n_local, rank, scale,...  82.2 us
    pallas_call x1, Pallas kernels, device_fn(): pl.pallas_call(functools.partial(backward_body, rank, scale), grid=(steps...  77.8 us
    pallas_call x1, Pallas kernels, device_fn(): pl.pallas_call(functools.partial(grads_body, scale, steps), grid=(steps +...  29.9 us
    all_to_all x2, starting transfers between devices, exchange(): return lax.all_to_all(arr, 'data', 0, 0, tiled=True)  5.99 us
  transfers between devices with their start and end apart: 2, of which 0 were waited for; matrix products, arithmetic and copies ran while one was open for 1% of the time, Pallas kernels for 54%

profile of v1, /device:TPU:0, one launch (start us, length us, event | category | flops | bytes accessed | tf_op | source)
XLA Modules:
  0.0 199.3 jit_solution(12052449860279305784)
XLA Ops:
  0.6 82.2 %forward.1 = (bf16[384,2048]{1,0:T(8,128)(2,1)}, bf16[384,2048]{1,0:T(8,128)(2,1)}, f32[384,8192]{1,0:T(8,128)}, f32[384,8192]{1,0:T(8,128)}, bf16[384,2048]{1,0...) custom-call(s32[1,128]{1,0:T(1,128)} %bitcast.47, ...), custom_call_target="tpu_custom_call" | custom-call | flops 50734301184 | bytes 125829120 | tf_op jit(solution)/shard_map/forward/pallas_call | solution.py:348
  82.8 3.1 %all-to-all-start = ((bf16[8,48,2048]{2,1,0:T(8,128)(2,1)}), bf16[8,48,2048]{2,1,0:T(8,128)(2,1)S(1)}, u32[]{:S(2)}, u32[]{:S(2)}) async-start(bf16[8,48,2048]{2,1,0:T(8,128)(2,1)} %bitcast.34), calls=%async_computation | async-start | bytes 3145728 | tf_op jit(solution)/shard_map/all_to_all | solution.py:328
  85.9 0.0 copy-start
  85.9 77.8 %backward.1 = (bf16[384,8192]{1,0:T(8,128)(2,1)}, bf16[384,8192]{1,0:T(8,128)(2,1)}, f32[512,8192]{1,0:T(8,128)}, bf16[384,2048]{1,0:T(8,128)(2,1)}, bf16[384,512]{1,0:T(8,128)(2,1)}, /*index=5*/bf16[384,512]{1,0:T(8,128)(2,1)}) custom-call(s32[384,1]{1,0:T(8,128)} %get-tuple-element.29.ids, bf16[384,2048]{1,0:T(8,128)(2,1)} %get-tuple-element.30.dy, ...), custom_call_target="tpu_custom_call" | custom-call | flops 53955526656 | bytes 125829120 | tf_op jit(solution)/shard_map/backward/pallas_call | solution.py:366
  163.7 0.0 copy-done
  163.7 0.0 all-to-all-done
  163.7 2.9 %all-to-all-start.1 = ((bf16[8,48,2048]{2,1,0:T(8,128)(2,1)}), bf16[8,48,2048]{2,1,0:T(8,128)(2,1)S(1)}, u32[]{:S(2)}, u32[]{:S(2)}) async-start(bf16[8,48,2048]{2,1,0:T(8,128)(2,1)} %bitcast.33), calls=%async_computation.1 | async-start | bytes 3145728 | tf_op jit(solution)/shard_map/all_to_all | solution.py:328
  166.7 0.2 convert_reduce_fusion
  166.8 29.9 %adapter_grads.1 = (f32[512,8192]{1,0:T(8,128)}, f32[512,8192]{1,0:T(8,128)}, f32[512,2048]{1,0:T(8,128)}, f32[512,2048]{1,0:T(8,128)}, f32[512,2048]{1,0:T(8,128)}) custom-call(bf16[384,512]{1,0:T(8,128)(2,1)} %get-tuple-element.34.pg, bf16[384,512]{1,0:T(8,128)(2,1)} %get-tuple-element.35.pu, bf16[384,512]{1,0:T(8,128)(2,1)} %get-tuple-element.36.pd, ...), custom_call_target="tpu_custom_call" | custom-call | flops 8858370048 | bytes 33554432 | tf_op jit(solution)/shard_map/adapter_grads/pallas_call | solution.py:382
  196.7 1.3 convolution_convert_fusion.1
  198.0 0.0 all-to-all-done.1
  198.0 1.3 convolution_convert_fusion
  (2 shorter events, 0.0 us)
Async XLA Ops:
  82.8 80.9 %all-to-all-start = ((bf16[8,48,2048]{2,1,0:T(8,128)(2,1)}), bf16[8,48,2048]{2,1,0:T(8,128)(2,1)S(1)}, u32[]{:S(2)}, u32[]{:S(2)}) async-start(bf16[8,48,2048]{2,1,0:T(8,128)(2,1)} %bitcast.34), calls=%async_computation | async-start | bytes 3145728 | tf_op jit(solution)/shard_map/all_to_all | solution.py:328
  85.9 77.8 %copy-start = (s32[128]{0:T(128)S(1)}, s32[128]{0:T(128)}, u32[]{:S(2)}) copy-start(s32[128]{0:T(128)} %param.13) | copy-start | bytes 1540
  163.7 34.3 %all-to-all-start.1 = ((bf16[8,48,2048]{2,1,0:T(8,128)(2,1)}), bf16[8,48,2048]{2,1,0:T(8,128)(2,1)S(1)}, u32[]{:S(2)}, u32[]{:S(2)}) async-start(bf16[8,48,2048]{2,1,0:T(8,128)(2,1)} %bitcast.33), calls=%async_computation.1 | async-start | bytes 3145728 | tf_op jit(solution)/shard_map/all_to_all | solution.py:328

commit v2 on v1

v2 whole, which is shorter than its diff:
```python
import functools

import jax
import jax.numpy as jnp
from jax import lax
from jax.experimental import pallas as pl
from jax.experimental.pallas import tpu as pltpu
from jax.sharding import PartitionSpec as P

LORA_ALPHA = 32
TILE = 512
WIDE = 1024
f32 = jnp.float32
bf = jnp.bfloat16


def mm(left, right, ldim=1, rdim=0):
    return lax.dot_general(left, right, (((ldim,), (rdim,)), ((), ())), preferred_element_type=f32)


def rounded(vals):
    return vals.astype(bf).astype(f32)


def keep(vals, ids, rank):
    cols = lax.div(lax.broadcasted_iota(jnp.int32, vals.shape, 1), jnp.int32(rank))
    return jnp.where(cols == ids, vals, 0.0).astype(bf)


def layer_body(cap, n_local, rank, scale, axes, ids_r, x_loc, dy_loc, ag_h, au_h, bd_h, wg, wu, wd, bg, bu, ad,
               x_o, dy_o, h_o, dg_o, du_o, dx_o, out_o, pack_o, pgt_o, put_o, qdt_o, pd_o, qg_o, qu_o,
               gu, x_own, dy_own, xs, dys, out_v, ids_s, ids_v, wbuf, bbuf, acc, qa, qb, pg, pu, qd, hbuf,
               send_sem, recv_sem, wsem, bsem, gsem, hsem, osem):
    group, dim = ids_s.shape[0], x_loc.shape[1]
    tokens, hidden = x_loc.shape[0], wg.shape[1]
    rows = group * cap
    n_slots, part = wbuf.shape[0], wbuf.shape[1]
    chunks = dim // part
    across = hidden // dim
    steps = hidden // part
    width = qa.shape[1]
    rep, me = lax.axis_index(axes[0]), lax.axis_index(axes[1])

    def peer(k):
        return lax.rem(me + k, group)

    barrier = pltpu.get_barrier_semaphore()
    for k in range(1, group):
        pl.semaphore_signal(barrier, inc=1, device_id=(rep, peer(k)), device_id_type=pl.DeviceIdType.MESH)

    def aligned(start, size, unit):
        return pl.ds(pl.multiple_of(start, unit), size)

    def start_tile(t, src):
        slot = lax.rem(t, n_slots)
        pltpu.make_async_copy(src, wbuf.at[slot], wsem.at[slot]).start()

    def wait_tile(t):
        slot = lax.rem(t, n_slots)
        pltpu.make_async_copy(bd_h, wbuf.at[slot], wsem.at[slot]).wait()
        return slot

    def block(ref, c, n):
        return ref.at[aligned(c * part, part, part), aligned(n * dim, dim, dim)]

    def start_pair(t, c, n):
        start_tile(t, block(wg, c, n))
        start_tile(t + 1, block(wu, c, n))

    def start_down(t, j):
        start_tile(t, wd.at[aligned(j * part, part, part)])

    def adapter_copies(j, slot):
        span = aligned(j * part, part, part)
        return [pltpu.make_async_copy(src.at[:, span], bbuf.at[slot, i], bsem.at[slot, i]) for i, src in enumerate((bg, bu, ad))]

    start_pair(0, 0, 0)
    start_pair(2, 0, 1)
    for j in range(2):
        for copy in adapter_copies(j, j):
            copy.start()

    ids = ids_r[...]
    owner = lax.div(ids, jnp.int32(n_local))
    local = lax.rem(ids, jnp.int32(n_local))
    owner_to = jnp.broadcast_to(owner.astype(f32), (tokens, tokens))
    earlier = lax.broadcasted_iota(jnp.int32, (tokens, tokens), 0) < lax.broadcasted_iota(jnp.int32, (tokens, tokens), 1)
    rank_in = jnp.sum(jnp.where((owner_to.T == owner_to) & earlier, 1.0, 0.0), axis=0, keepdims=True).astype(jnp.int32)
    pack = jnp.where(lax.broadcasted_iota(jnp.int32, (rows, tokens), 0) == owner * cap + rank_in, 1.0, 0.0).astype(bf)
    pack_o[...] = pack
    lanes = 128
    spread = jnp.where(lax.broadcasted_iota(jnp.int32, (group * lanes, tokens), 0) == owner * lanes + rank_in, 1.0, 0.0).astype(bf)
    tagged = mm(jnp.broadcast_to((local + 1).astype(f32), (8, tokens)).astype(bf), spread, 1, 1)
    for d in range(group):
        ids_s[d] = tagged[:, d * lanes:(d + 1) * lanes]

    def pack_part(src, dst, c):
        span = slice(c * part, (c + 1) * part)
        dst[:, span] = mm(pack, src[:, span]).astype(bf)

    mine = aligned(me * cap, cap, 16)

    def row_copy(src, dst, span, c, k):
        return pltpu.make_async_remote_copy(
            src_ref=src.at[aligned(peer(k) * cap, cap, 16), span], dst_ref=dst.at[mine, span],
            send_sem=send_sem.at[c, k], recv_sem=recv_sem.at[c, k],
            device_id=(rep, peer(k)), device_id_type=pl.DeviceIdType.MESH)

    def id_copy(k):
        return pltpu.make_async_remote_copy(
            src_ref=ids_s.at[peer(k)], dst_ref=ids_v.at[me], send_sem=send_sem.at[chunks + 1, k], recv_sem=recv_sem.at[chunks + 1, k],
            device_id=(rep, peer(k)), device_id_type=pl.DeviceIdType.MESH)

    others = range(1, group)
    x_copies = [[row_copy(xs, x_own, pl.ds(c * part, part), c, k) for k in others] for c in range(chunks)]
    dy_copies = [row_copy(dys, dy_own, pl.ds(0, dim), chunks, k) for k in others]
    id_copies = [id_copy(k) for k in others]
    out_copies = [row_copy(xs, out_v, pl.ds(0, dim), chunks + 2, k) for k in others]

    pack_part(x_loc, xs, 0)
    pl.semaphore_wait(barrier, group - 1)
    for c in range(chunks):
        if c + 1 < chunks:
            pack_part(x_loc, xs, c + 1)
        for copy in x_copies[c]:
            copy.start()
    for copy in id_copies:
        copy.start()
    for c in range(chunks):
        pack_part(dy_loc, dys, c)
    x_own[mine, :] = xs[mine, :]
    dy_own[mine, :] = dys[mine, :]
    ids_v[me] = ids_s[me]
    for copy in dy_copies:
        copy.start()

    def clear(i, carry):
        gu[0, aligned(i * 8, 8, 8), :] = jnp.zeros((8, hidden), f32)
        gu[1, aligned(i * 8, 8, 8), :] = jnp.zeros((8, hidden), f32)
        return carry

    lax.fori_loop(0, rows // 8, clear, 0)
    acc[...] = jnp.zeros_like(acc)
    qa[...] = jnp.zeros_like(qa)
    qb[...] = jnp.zeros_like(qb)

    pairs = chunks * across
    for c in range(chunks):
        for copy in x_copies[c]:
            copy.wait_recv()

        def pre_step(n, carry):
            p = c * across + n
            ahead = p + 2

            @pl.when(ahead < pairs)
            def _():
                start_pair(2 * ahead, lax.div(ahead, across), lax.rem(ahead, across))

            if c == chunks - 1:
                @pl.when(ahead == pairs)
                def _():
                    start_tile(2 * pairs, ag_h)
                    start_tile(2 * pairs + 1, au_h)

                @pl.when(ahead == pairs + 1)
                def _():
                    start_down(2 * pairs + 2, 0)
                    start_down(2 * pairs + 3, 1)

            span = aligned(n * dim, dim, dim)
            one, two = wait_tile(2 * p), wait_tile(2 * p + 1)
            gu[0, :, span] += mm(x_own[:, c * part:(c + 1) * part], wbuf[one])
            gu[1, :, span] += mm(x_own[:, c * part:(c + 1) * part], wbuf[two])
            return carry

        lax.fori_loop(0, across, pre_step, 0)

    base = 2 * pairs
    start_down(base + 4, 2)
    start_down(base + 5, 3)
    for copy in id_copies:
        copy.wait_recv()
    got = jnp.concatenate([ids_v[s, 0:1, :] for s in range(group)] + [jnp.zeros((lanes - group, lanes), f32)], axis=0).T
    ids_col = jnp.concatenate([got[0:cap, s:s + 1] for s in range(group)], axis=0).astype(jnp.int32) - 1
    x_out = pltpu.make_async_copy(x_own, x_o, osem.at[0])
    x_out.start()
    one, two = wait_tile(base), wait_tile(base + 1)
    pg[...] = keep(mm(x_own[...], wbuf[one], 1, 1), ids_col, rank)
    pu[...] = keep(mm(x_own[...], wbuf[two], 1, 1), ids_col, rank)
    base += 2

    def h_copy(j, two):
        return pltpu.make_async_copy(hbuf.at[two], h_o.at[:, aligned(j * part, part, part)], hsem.at[two])

    def step(j, carry):
        t = base + j

        @pl.when(j + 4 < steps)
        def _():
            start_down(t + 4, j + 4)

        @pl.when(j + 4 == steps)
        def _():
            start_tile(t + 4, bd_h)

        @pl.when(j + 4 > steps)
        def _():
            start_down(t + 4, j + 3 - steps)

        span = aligned(j * part, part, part)
        two = lax.rem(j, 2)

        @pl.when(j >= 2)
        def _():
            h_copy(0, two).wait()

        for copy in adapter_copies(0, two):
            copy.wait()
        slot = wait_tile(t)
        gate = gu[0, :, span] + rounded(scale * mm(pg[...], bbuf[two, 0]))
        up = gu[1, :, span] + rounded(scale * mm(pu[...], bbuf[two, 1]))
        gu[0, :, span] = gate
        gu[1, :, span] = up
        h = (gate * jax.nn.sigmoid(gate) * up).astype(bf)
        hbuf[two] = h
        slab = aligned(lax.rem(j, width // lanes) * lanes, lanes, lanes)
        pgt_o[slab, :] = pg[:, slab].T
        put_o[slab, :] = pu[:, slab].T
        acc[...] += mm(h, wbuf[slot])
        qa[...] += mm(h, bbuf[two, 2], 1, 1)
        h_copy(j, two).start()
        for copy in adapter_copies(lax.rem(j + 2, steps), two):
            copy.start()
        return carry

    lax.fori_loop(0, steps, step, 0)
    for two in range(2):
        h_copy(0, two).wait()
    base += steps
    start_down(base + 4, 3)
    for copy in dy_copies:
        copy.wait_recv()
    dy_out = pltpu.make_async_copy(dy_own, dy_o, osem.at[1])
    dy_out.start()
    for copies in x_copies:
        for copy in copies:
            copy.wait_send()
    slot = wait_tile(base)
    pd = keep(qa[...], ids_col, rank)
    pd_o[...] = pd
    xs[...] = (x_own[...].astype(f32) + acc[...] + rounded(scale * mm(pd, wbuf[slot]))).astype(bf)
    qd[...] = keep(scale * mm(dy_own[...], wbuf[slot], 1, 1), ids_col, rank)
    for copy in out_copies:
        copy.start()
    out_v[mine, :] = xs[mine, :]
    acc[...] = jnp.zeros_like(acc)
    qa[...] = jnp.zeros_like(qa)
    base += 1
    x_out.wait()
    for copy in dy_copies:
        copy.wait_send()

    per = dim // part
    width_tiles = 3 * per

    def grad_copies(j, i):
        span = aligned(j * part, part, part)
        here = aligned(i * part, part, part)
        return [pltpu.make_async_copy(src.at[:, here], dst.at[:, span], gsem.at[i, n])
                for n, (src, dst) in enumerate(((x_own, dg_o), (dys, du_o)))]

    def super_step(s, carry):
        first = base + s * width_tiles

        def sub_step(k, carry):
            start_pair(first + per + 2 * k, k, s)
            for ii in range(2):
                i = 2 * k + ii
                j = s * per + i
                span = aligned(j * part, part, part)
                here = aligned(i * part, part, part)

                @pl.when(s > 0)
                def _():
                    for copy in grad_copies(0, i):
                        copy.wait()

                for copy in adapter_copies(0, ii):
                    copy.wait()
                slot = wait_tile(first + i)
                gate, up = gu[0, :, span], gu[1, :, span]
                sig = jax.nn.sigmoid(gate)
                act = gate * sig
                dh = mm(dy_own[...], wbuf[slot], 1, 1) + rounded(mm(qd[...], bbuf[ii, 2]))
                dg = (dh * up * sig * (1.0 + gate * (1.0 - sig))).astype(bf)
                du = (dh * act).astype(bf)
                x_own[:, here] = dg
                dys[:, here] = du
                slab = aligned(lax.rem(j, width // lanes) * lanes, lanes, lanes)
                qdt_o[slab, :] = qd[:, slab].T
                qa[...] += mm(dg, bbuf[ii, 0], 1, 1)
                qb[...] += mm(du, bbuf[ii, 1], 1, 1)
                for copy in grad_copies(j, i):
                    copy.start()

                @pl.when(j + 2 < steps)
                def _():
                    for copy in adapter_copies(j + 2, ii):
                        copy.start()

            return carry

        lax.fori_loop(0, per // 2, sub_step, 0)

        def dx_step(d, carry):
            t = first + per + 2 * d

            @pl.when(d < per - 2)
            def _():
                start_pair(t + 4, d + 2, s)

            @pl.when((d >= per - 2) & (s < across - 1))
            def _():
                j = (s + 1) * per + 2 * (d - (per - 2))
                start_down(t + 4, j)
                start_down(t + 5, j + 1)

            @pl.when((d == per - 2) & (s == across - 1))
            def _():
                start_tile(t + 4, ag_h)
                start_tile(t + 5, au_h)

            here = aligned(d * part, part, part)
            one, two = wait_tile(t), wait_tile(t + 1)
            acc[:, here] += mm(x_own[...], wbuf[one], 1, 1) + mm(dys[...], wbuf[two], 1, 1)
            return carry

        lax.fori_loop(0, per, dx_step, 0)
        return carry

    lax.fori_loop(0, across, super_step, 0)
    base += across * width_tiles
    one, two = wait_tile(base), wait_tile(base + 1)
    qg = keep(scale * qa[...], ids_col, rank)
    qu = keep(scale * qb[...], ids_col, rank)
    qg_o[...] = qg
    qu_o[...] = qu
    lora = rounded(mm(qg, wbuf[one]) + mm(qu, wbuf[two]))
    for i in range(per):
        for copy in grad_copies(0, i):
            copy.wait()
    dys[...] = (dy_own[...].astype(f32) + acc[...] + lora).astype(bf)
    dx_out = pltpu.make_async_copy(dys, dx_o, osem.at[2])
    dx_out.start()
    for copy in out_copies:
        copy.wait_recv()
    out_o[...] = mm(pack_o[...], out_v[...], 0, 0).astype(bf)
    for copies in (id_copies, out_copies):
        for copy in copies:
            copy.wait_send()
    dy_out.wait()
    dx_out.wait()


def grads_body(scale, wide, pgt, put, qdt, pd, qg, qu, x, dy, h, dg, du, gbg, gbu, gad, gag, gau, gbd, pdt, qgt, qut):
    step = pl.program_id(0)

    @pl.when(step == wide)
    def _():
        for src, dst in ((pd, pdt), (qg, qgt), (qu, qut)):
            dst[...] = src[...].T

    @pl.when(step < wide)
    def _():
        gbg[...] = scale * mm(pgt[...], dg[...])
        gbu[...] = scale * mm(put[...], du[...])
        gad[...] = mm(qdt[...], h[...])

    @pl.when(step >= wide)
    def _():
        gag[...] = mm(qgt[...], x[...])
        gau[...] = mm(qut[...], x[...])
        gbd[...] = scale * mm(pdt[...], dy[...])


def whole(shape):
    return pl.BlockSpec(shape, lambda j: (0, 0), pipeline_mode=pl.Buffered(1))


def params():
    return pltpu.CompilerParams(dimension_semantics=('arbitrary',), vmem_limit_bytes=60 * 2 ** 20)


def cost(flops, nbytes):
    return pl.CostEstimate(flops=flops, bytes_accessed=nbytes, transcendentals=0)


def solution(mesh):
    group = mesh.shape['data']
    tok_spec = P(('rep', 'data'), None)
    id_spec = P(('rep', 'data'))
    full_spec = P(None, None)
    own_spec = P('data', None, None)
    grad_spec = P(('rep', 'data'), None, None)

    def device_fn(x_loc, ids_loc, dy_loc, w_gate, w_up, w_down, a_gate, b_gate, a_up, b_up, a_down, b_down):
        tokens, dim = x_loc.shape
        n_local, _, rank = a_gate.shape
        hidden = w_gate.shape[1]
        width = n_local * rank
        scale = LORA_ALPHA / rank
        cap = ((3 * tokens + 8 * group - 1) // (8 * group)) * 8
        rows = group * cap
        steps = hidden // TILE

        def exchange(arr):
            return lax.all_to_all(arr, 'data', 0, 0, tiled=True)

        def as_rows(weight):
            return jnp.swapaxes(weight, 1, 2).reshape(width, weight.shape[1])

        ag, au, ad = as_rows(a_gate), as_rows(a_up), as_rows(a_down)
        bg, bu, bd = b_gate.reshape(width, hidden), b_up.reshape(width, hidden), b_down.reshape(width, dim)

        def arr(shape, dtype):
            return jax.ShapeDtypeStruct(shape, dtype)

        base = 2 * rows * dim * hidden
        lora = 2 * rows * width * hidden
        small = 2 * rows * width * dim
        chunks = dim // TILE
        any_spec = pl.BlockSpec(memory_space=pl.ANY)
        vmem_spec = pl.BlockSpec(memory_space=pltpu.VMEM)
        sem = pltpu.SemaphoreType.DMA
        x, dy, h, dg, du, dx, out, pack, pgt, put, qdt, pd, qg, qu = pl.pallas_call(
            functools.partial(layer_body, cap, n_local, rank, scale, mesh.axis_names),
            in_specs=[vmem_spec] * 3 + [any_spec] * 9,
            out_specs=[any_spec] * 6 + [vmem_spec] * 8,
            out_shape=[arr((rows, dim), bf)] * 2 + [arr((rows, hidden), bf)] * 3 + [arr((rows, dim), bf), arr((tokens, dim), bf), arr((rows, tokens), bf)]
            + [arr((width, rows), bf)] * 3 + [arr((rows, width), bf)] * 3,
            scratch_shapes=[
                pltpu.VMEM((2, rows, hidden), f32),
                pltpu.VMEM((rows, dim), bf), pltpu.VMEM((rows, dim), bf), pltpu.VMEM((rows, dim), bf), pltpu.VMEM((rows, dim), bf),
                pltpu.VMEM((rows, dim), bf),
                pltpu.VMEM((group, 8, 128), f32), pltpu.VMEM((group, 8, 128), f32),
                pltpu.VMEM((6, TILE, dim), bf), pltpu.VMEM((2, 3, width, TILE), bf),
                pltpu.VMEM((rows, dim), f32), pltpu.VMEM((rows, width), f32), pltpu.VMEM((rows, width), f32),
                pltpu.VMEM((rows, width), bf), pltpu.VMEM((rows, width), bf), pltpu.VMEM((rows, width), bf), pltpu.VMEM((2, rows, TILE), bf),
                sem((chunks + 3, group)), sem((chunks + 3, group)), sem((6,)), sem((2, 3)), sem((dim // TILE, 2)), sem((2,)), sem((3,)),
            ],
            compiler_params=pltpu.CompilerParams(collective_id=0, has_side_effects=True, vmem_limit_bytes=67043328),
            cost_estimate=cost(6 * base + 6 * lora + 6 * small, 12 * dim * hidden),
            name='layer',
        )(ids_loc[None, :], x_loc, dy_loc, ag, au, bd, w_gate, w_up, w_down, bg, bu, ad)
        steps = hidden // WIDE
        wide_cols = pl.BlockSpec((rows, WIDE), lambda j: (0, jnp.minimum(j, steps - 1)))
        wide_grad = pl.BlockSpec((width, WIDE), lambda j: (0, jnp.minimum(j, steps - 1)))
        slim_cols = pl.BlockSpec((rows, TILE), lambda j: (0, jnp.maximum(j - steps, 0)))
        slim_grad = pl.BlockSpec((width, TILE), lambda j: (0, jnp.maximum(j - steps, 0)))
        g_bg, g_bu, g_ad, g_ag, g_au, g_bd = pl.pallas_call(
            functools.partial(grads_body, scale, steps),
            grid=(steps + dim // TILE,),
            in_specs=[whole((width, rows))] * 3 + [whole((rows, width))] * 3 + [slim_cols, slim_cols, wide_cols, wide_cols, wide_cols],
            out_specs=[wide_grad, wide_grad, wide_grad, slim_grad, slim_grad, slim_grad],
            out_shape=[arr((width, hidden), f32)] * 3 + [arr((width, dim), f32)] * 3,
            scratch_shapes=[pltpu.VMEM((width, rows), bf)] * 3,
            compiler_params=params(),
            cost_estimate=cost(3 * lora + 3 * small, 12 * width * hidden),
            name='adapter_grads',
        )(pgt, put, qdt, pd, qg, qu, x, dy, h, dg, du)

        def back(vals):
            return mm(pack, exchange(vals), 0, 0).astype(bf)

        def a_grad(vals):
            return jnp.swapaxes(vals.reshape(n_local, rank, vals.shape[1]), 1, 2)

        def b_grad(vals):
            return vals.reshape(n_local, rank, vals.shape[1])

        return out, back(dx), a_grad(g_ag), b_grad(g_bg), a_grad(g_au), b_grad(g_bu), a_grad(g_ad), b_grad(g_bd)

    return jax.shard_map(
        device_fn,
        mesh=mesh,
        in_specs=(tok_spec, id_spec, tok_spec, full_spec, full_spec, full_spec) + (own_spec,) * 6,
        out_specs=(tok_spec, tok_spec) + (grad_spec,) * 6,
        check_vma=False,
    )
```

time: 200 us -> 180 us (0.900)
  Pallas kernels: 190 us -> 173 us
  starting transfers between devices: 5.99 us -> 2.81 us
    pallas_call x2 -> x1, Pallas kernels: 160 us -> 139 us  [device_fn(): pl.pallas_call(functools.partial(layer_body, cap, n_local, rank, scale, m...]
    pallas_call x1, Pallas kernels: 29.9 us -> 33.7 us  [device_fn(): pl.pallas_call(functools.partial(grads_body, scale, steps), grid=(steps +...]
    all_to_all x2 -> x1, starting transfers between devices: 5.99 us -> 2.81 us  [exchange(): return lax.all_to_all(arr, 'data', 0, 0, tiled=True)]
  transfers between devices with their start and end apart: 2 -> 1, of which waited for: 0 -> 0; matrix products, arithmetic and copies ran while one was open for 1% -> 0% of each run, Pallas kernels for 54% -> 19%
where the time goes in v2:
time: 180 us; the launch traced here: 178 us
  Pallas kernels  173 us (96%)
  starting transfers between devices  2.81 us (2%)
    pallas_call x1, Pallas kernels, device_fn(): pl.pallas_call(functools.partial(layer_body, cap, n_local, rank, scale, m...  139 us
    pallas_call x1, Pallas kernels, device_fn(): pl.pallas_call(functools.partial(grads_body, scale, steps), grid=(steps +...  33.7 us
  transfers between devices with their start and end apart: 1, of which 0 were waited for; matrix products, arithmetic and copies ran while one was open for 0% of the time, Pallas kernels for 19%

profile of v2, /device:TPU:0, one launch (start us, length us, event | category | flops | bytes accessed | tf_op | source)
XLA Modules:
  0.0 178.4 jit_solution(10466347880034970038)
XLA Ops:
  0.6 139.2 %layer.1 = (bf16[384,2048]{1,0:T(8,128)(2,1)}, bf16[384,2048]{1,0:T(8,128)(2,1)}, bf16[384,8192]{1,0:T(8,128)(2,1)}, bf16[384,8192]{1,0:T(8,128)(2,1)}, bf16[384...) custom-call(s32[1,128]{1,0:T(1,128)} %bitcast.37, ...), custom_call_target="tpu_custom_call" | custom-call | flops 101468602368 | bytes 201326592 | tf_op jit(solution)/shard_map/layer/pallas_call | solution.py:436
  139.9 2.8 %all-to-all-start = ((bf16[8,48,2048]{2,1,0:T(8,128)(2,1)}), bf16[8,48,2048]{2,1,0:T(8,128)(2,1)S(1)}, u32[]{:S(2)}, u32[]{:S(2)}) async-start(bf16[8,48,2048]{2,1,0:T(8,128)(2,1)} %bitcast.30), calls=%async_computation | async-start | bytes 3145728 | tf_op jit(solution)/shard_map/all_to_all | solution.py:418
  142.7 0.0 copy-start.1
  142.7 0.0 copy-start
  142.7 33.7 %adapter_grads.1 = (f32[512,8192]{1,0:T(8,128)}, f32[512,8192]{1,0:T(8,128)}, f32[512,8192]{1,0:T(8,128)}, f32[512,2048]{1,0:T(8,128)}, f32[512,2048]{1,0:T(8,128)}, /*index=5*/f32[512,2048]{1,0:T(8,128)}) custom-call(bf16[512,384]{1,0:T(8,128)(2,1)} %get-tuple-element.31.pgt, bf16[512,384]{1,0:T(8,128)(2,1)} %get-tuple-element.32.put, ...), custom_call_target="tpu_custom_call" | custom-call | flops 12079595520 | bytes 50331648 | tf_op jit(solution)/shard_map/adapter_grads/pallas_call | solution.py:461
  176.3 0.0 all-to-all-done
  176.3 0.0 copy-done.1
  176.4 1.3 convolution_convert_fusion
  177.6 0.0 copy-done
  177.6 0.8 copy.21
Async XLA Ops:
  139.9 36.5 %all-to-all-start = ((bf16[8,48,2048]{2,1,0:T(8,128)(2,1)}), bf16[8,48,2048]{2,1,0:T(8,128)(2,1)S(1)}, u32[]{:S(2)}, u32[]{:S(2)}) async-start(bf16[8,48,2048]{2,1,0:T(8,128)(2,1)} %bitcast.30), calls=%async_computation | async-start | bytes 3145728 | tf_op jit(solution)/shard_map/all_to_all | solution.py:418
  142.7 33.7 %copy-start.1 = (bf16[384,128]{1,0:T(8,128)(2,1)S(1)}, bf16[384,128]{1,0:T(8,128)(2,1)}, u32[]{:S(2)}) copy-start(bf16[384,128]{1,0:T(8,128)(2,1)} %get-tuple-element.29) | copy-start | bytes 294916
  142.7 35.0 %copy-start = (bf16[128,2048]{1,0:T(8,128)(2,1)S(1)}, bf16[128,2048]{1,0:T(8,128)(2,1)}, u32[]{:S(2)}) copy-start(bf16[128,2048]{1,0:T(8,128)(2,1)} %get-tuple-element.56) | copy-start | bytes 1572868

commit v3 on v2

--- a/solution.py
+++ b/solution.py
@@ -9,7 +9,7 @@
 
 LORA_ALPHA = 32
 TILE = 512
-WIDE = 1024
+DEEP = 4
 f32 = jnp.float32
 bf = jnp.bfloat16
 
@@ -29,7 +29,7 @@
 
 def layer_body(cap, n_local, rank, scale, axes, ids_r, x_loc, dy_loc, ag_h, au_h, bd_h, wg, wu, wd, bg, bu, ad,
                x_o, dy_o, h_o, dg_o, du_o, dx_o, out_o, pack_o, pgt_o, put_o, qdt_o, pd_o, qg_o, qu_o,
-               gu, x_own, dy_own, xs, dys, out_v, ids_s, ids_v, wbuf, bbuf, acc, qa, qb, pg, pu, qd, hbuf,
+               gu, x_own, dy_own, xs, dys, out_v, ids_s, ids_v, wbuf, bbuf, acc, qa, qb, pg, pu, qd,
                send_sem, recv_sem, wsem, bsem, gsem, hsem, osem):
     group, dim = ids_s.shape[0], x_loc.shape[1]
     tokens, hidden = x_loc.shape[0], wg.shape[1]
@@ -74,11 +74,25 @@
         span = aligned(j * part, part, part)
         return [pltpu.make_async_copy(src.at[:, span], bbuf.at[slot, i], bsem.at[slot, i]) for i, src in enumerate((bg, bu, ad))]
 
+    def adapter_copy(j, slot, i):
+        span = aligned(j * part, part, part)
+        return pltpu.make_async_copy((bg, bu, ad)[i].at[:, span], bbuf.at[slot, i], bsem.at[slot, i])
+
+    def refill(j, which):
+        for ii in range(2):
+            for i in which:
+                adapter_copy(lax.rem(j + 2 + ii, steps), ii, i).start()
+
+    def wait_adapters(which):
+        for ii in range(2):
+            for i in which:
+                adapter_copy(0, ii, i).wait()
+
     start_pair(0, 0, 0)
     start_pair(2, 0, 1)
     for j in range(2):
-        for copy in adapter_copies(j, j):
-            copy.start()
+        for i in range(3):
+            adapter_copy(j, j, i).start()
 
     ids = ids_r[...]
     owner = lax.div(ids, jnp.int32(n_local))
@@ -149,32 +163,35 @@
         for copy in x_copies[c]:
             copy.wait_recv()
 
-        def pre_step(n, carry):
-            p = c * across + n
-            ahead = p + 2
-
-            @pl.when(ahead < pairs)
-            def _():
-                start_pair(2 * ahead, lax.div(ahead, across), lax.rem(ahead, across))
-
-            if c == chunks - 1:
-                @pl.when(ahead == pairs)
-                def _():
-                    start_tile(2 * pairs, ag_h)
-                    start_tile(2 * pairs + 1, au_h)
-
-                @pl.when(ahead == pairs + 1)
-                def _():
+        last = c == chunks - 1
+
+        def ahead(p):
+            start_pair(2 * p, lax.div(p, across), lax.rem(p, across))
+
+        def pre_step(i, carry, last_step=False):
+            p = c * across + 2 * i
+            if last_step:
+                start_tile(2 * pairs, ag_h)
+                start_tile(2 * pairs + 1, au_h)
+            else:
+                ahead(p + 2)
+            for half in range(2):
+                t = 2 * (p + half)
+                span = aligned((2 * i + half) * dim, dim, dim)
+                one, two = wait_tile(t), wait_tile(t + 1)
+                gu[0, :, span] += mm(x_own[:, c * part:(c + 1) * part], wbuf[one])
+                gu[1, :, span] += mm(x_own[:, c * part:(c + 1) * part], wbuf[two])
+                if half == 0 and last_step:
                     start_down(2 * pairs + 2, 0)
                     start_down(2 * pairs + 3, 1)
-
-            span = aligned(n * dim, dim, dim)
-            one, two = wait_tile(2 * p), wait_tile(2 * p + 1)
-            gu[0, :, span] += mm(x_own[:, c * part:(c + 1) * part], wbuf[one])
-            gu[1, :, span] += mm(x_own[:, c * part:(c + 1) * part], wbuf[two])
+                elif half == 0:
+                    ahead(p + 3)
             return carry
 
-        lax.fori_loop(0, across, pre_step, 0)
+        turns = across // 2
+        lax.fori_loop(0, turns - 1 if last else turns, pre_step, 0)
+        if last:
+            pre_step(turns - 1, 0, True)
 
     base = 2 * pairs
     start_down(base + 4, 2)
@@ -191,50 +208,59 @@
     base += 2
 
     def h_copy(j, two):
-        return pltpu.make_async_copy(hbuf.at[two], h_o.at[:, aligned(j * part, part, part)], hsem.at[two])
-
-    def step(j, carry):
+        return pltpu.make_async_copy(dys.at[:, pl.ds(two * part, part)], h_o.at[:, aligned(j * part, part, part)], hsem.at[two])
+
+    for copy in dy_copies:
+        copy.wait_send()
+
+    def step(jj, carry):
+        j = 2 * jj
         t = base + j
 
         @pl.when(j + 4 < steps)
         def _():
             start_down(t + 4, j + 4)
+            start_down(t + 5, j + 5)
 
         @pl.when(j + 4 == steps)
         def _():
             start_tile(t + 4, bd_h)
+            start_down(t + 5, 0)
 
         @pl.when(j + 4 > steps)
         def _():
-            start_down(t + 4, j + 3 - steps)
-
-        span = aligned(j * part, part, part)
-        two = lax.rem(j, 2)
-
-        @pl.when(j >= 2)
+            start_down(t + 4, 1)
+            start_down(t + 5, 2)
+
+        @pl.when(jj > 0)
         def _():
-            h_copy(0, two).wait()
-
-        for copy in adapter_copies(0, two):
-            copy.wait()
-        slot = wait_tile(t)
-        gate = gu[0, :, span] + rounded(scale * mm(pg[...], bbuf[two, 0]))
-        up = gu[1, :, span] + rounded(scale * mm(pu[...], bbuf[two, 1]))
-        gu[0, :, span] = gate
-        gu[1, :, span] = up
-        h = (gate * jax.nn.sigmoid(gate) * up).astype(bf)
-        hbuf[two] = h
-        slab = aligned(lax.rem(j, width // lanes) * lanes, lanes, lanes)
+            for ii in range(2):
+                h_copy(0, ii).wait()
+
+        wait_adapters((0, 1))
+        slots = [wait_tile(t), wait_tile(t + 1)]
+        for ii in range(2):
+            span = aligned((j + ii) * part, part, part)
+            gate = gu[0, :, span] + rounded(scale * mm(pg[...], bbuf[ii, 0]))
+            up = gu[1, :, span] + rounded(scale * mm(pu[...], bbuf[ii, 1]))
+            gu[0, :, span] = gate
+            gu[1, :, span] = up
+            dys[:, ii * part:(ii + 1) * part] = (gate * jax.nn.sigmoid(gate) * up).astype(bf)
+        refill(j, (0, 1))
+        for ii in range(2):
+            h_copy(j + ii, ii).start()
+        slab = aligned(lax.rem(jj, width // lanes) * lanes, lanes, lanes)
         pgt_o[slab, :] = pg[:, slab].T
         put_o[slab, :] = pu[:, slab].T
-        acc[...] += mm(h, wbuf[slot])
-        qa[...] += mm(h, bbuf[two, 2], 1, 1)
-        h_copy(j, two).start()
-        for copy in adapter_copies(lax.rem(j + 2, steps), two):
-            copy.start()
+        wait_adapters((2,))
+        for ii in range(2):
+            h = dys[:, ii * part:(ii + 1) * part]
+            acc[...] += mm(h, wbuf[slots[ii]])
+            qa[...] += mm(h, bbuf[ii, 2], 1, 1)
+        refill(j, (2,))
         return carry
 
-    lax.fori_loop(0, steps, step, 0)
+    lax.fori_loop(0, steps // 2, step, 0)
     for two in range(2):
         h_copy(0, two).wait()
     base += steps
@@ -258,8 +284,6 @@
     qa[...] = jnp.zeros_like(qa)
     base += 1
     x_out.wait()
-    for copy in dy_copies:
-        copy.wait_send()
 
     per = dim // part
     width_tiles = 3 * per
@@ -274,74 +298,77 @@
         first = base + s * width_tiles
 
         def sub_step(k, carry):
-            start_pair(first + per + 2 * k, k, s)
+            i0 = 2 * k
+            j0 = s * per + i0
+            start_pair(first + per + i0, k, s)
+
+            @pl.when(s > 0)
+            def _():
+                for ii in range(2):
+                    for copy in grad_copies(0, i0 + ii):
+                        copy.wait()
+
+            wait_adapters((2,))
+            slots = [wait_tile(first + i0), wait_tile(first + i0 + 1)]
             for ii in range(2):
-                i = 2 * k + ii
-                j = s * per + i
-                span = aligned(j * part, part, part)
-                here = aligned(i * part, part, part)
-
-                @pl.when(s > 0)
-                def _():
-                    for copy in grad_copies(0, i):
-                        copy.wait()
-
-                for copy in adapter_copies(0, ii):
-                    copy.wait()
-                slot = wait_tile(first + i)
+                span = aligned((j0 + ii) * part, part, part)
+                here = aligned((i0 + ii) * part, part, part)
                 gate, up = gu[0, :, span], gu[1, :, span]
                 sig = jax.nn.sigmoid(gate)
                 act = gate * sig
-                dh = mm(dy_own[...], wbuf[slot], 1, 1) + rounded(mm(qd[...], bbuf[ii, 2]))
-                dg = (dh * up * sig * (1.0 + gate * (1.0 - sig))).astype(bf)
-                du = (dh * act).astype(bf)
-                x_own[:, here] = dg
-                dys[:, here] = du
-                slab = aligned(lax.rem(j, width // lanes) * lanes, lanes, lanes)
-                qdt_o[slab, :] = qd[:, slab].T
-                qa[...] += mm(dg, bbuf[ii, 0], 1, 1)
-                qb[...] += mm(du, bbuf[ii, 1], 1, 1)
-                for copy in grad_copies(j, i):
+                dh = mm(dy_own[...], wbuf[slots[ii]], 1, 1) + rounded(mm(qd[...], bbuf[ii, 2]))
+                x_own[:, here] = (dh * up * sig * (1.0 + gate * (1.0 - sig))).astype(bf)
+                dys[:, here] = (dh * act).astype(bf)
+            refill(j0, (2,))
+            slab = aligned(lax.rem(lax.div(j0, 2), width // lanes) * lanes, lanes, lanes)
+            qdt_o[slab, :] = qd[:, slab].T
+            wait_adapters((0, 1))
+            for ii in range(2):
+                here = aligned((i0 + ii) * part, part, part)
+                qa[...] += mm(x_own[:, here], bbuf[ii, 0], 1, 1)
+                qb[...] += mm(dys[:, here], bbuf[ii, 1], 1, 1)
+                for copy in grad_copies(j0 + ii, i0 + ii):
                     copy.start()
-
-                @pl.when(j + 2 < steps)
+            refill(j0, (0, 1))
+            return carry
+
+        lax.fori_loop(0, per // 2, sub_step, 0)
+
+        for turn in range(per // 2):
+            final = turn == per // 2 - 1
+            t0 = first + per + 4 * turn
+            nxt = jnp.minimum((s + 1) * per, steps - per)
+            if final:
+                @pl.when(s < across - 1)
                 def _():
-                    for copy in adapter_copies(j + 2, ii):
-                        copy.start()
-
-            return carry
-
-        lax.fori_loop(0, per // 2, sub_step, 0)
-
-        def dx_step(d, carry):
-            t = first + per + 2 * d
-
-            @pl.when(d < per - 2)
-            def _():
-                start_pair(t + 4, d + 2, s)
-
-            @pl.when((d >= per - 2) & (s < across - 1))
-            def _():
-                j = (s + 1) * per + 2 * (d - (per - 2))
-                start_down(t + 4, j)
-                start_down(t + 5, j + 1)
-
-            @pl.when((d == per - 2) & (s == across - 1))
-            def _():
-                start_tile(t + 4, ag_h)
-                start_tile(t + 5, au_h)
-
-            here = aligned(d * part, part, part)
-            one, two = wait_tile(t), wait_tile(t + 1)
-            acc[:, here] += mm(x_own[...], wbuf[one], 1, 1) + mm(dys[...], wbuf[two], 1, 1)
-            return carry
-
-        lax.fori_loop(0, per, dx_step, 0)
+                    start_down(t0 + 4, nxt)
+                    start_down(t0 + 5, nxt + 1)
+
+                @pl.when(s == across - 1)
+                def _():
+                    start_tile(t0 + 4, ag_h)
+                    start_tile(t0 + 5, au_h)
+            else:
+                start_pair(t0 + 4, 2 * turn + 2, s)
+            for half in range(2):
+                d = 2 * turn + half
+                t = t0 + 2 * half
+                here = slice(d * part, (d + 1) * part)
+                one, two = wait_tile(t), wait_tile(t + 1)
+                acc[:, here] += mm(x_own[...], wbuf[one], 1, 1) + mm(dys[...], wbuf[two], 1, 1)
+                if half == 0 and final:
+                    start_down(t0 + 6, nxt + 2)
+                    start_down(t0 + 7, nxt + 3)
+                elif half == 0:
+                    start_pair(t0 + 6, 2 * turn + 3, s)
         return carry
 
     lax.fori_loop(0, across, super_step, 0)
     base += across * width_tiles
     one, two = wait_tile(base), wait_tile(base + 1)
+    wait_tile(base + 2)
+    wait_tile(base + 3)
+    wait_adapters((0, 1, 2))
     qg = keep(scale * qa[...], ids_col, rank)
     qu = keep(scale * qb[...], ids_col, rank)
     qg_o[...] = qg
@@ -363,33 +390,78 @@
     dx_out.wait()
 
 
-def grads_body(scale, wide, pgt, put, qdt, pd, qg, qu, x, dy, h, dg, du, gbg, gbu, gad, gag, gau, gbd, pdt, qgt, qut):
-    step = pl.program_id(0)
-
-    @pl.when(step == wide)
-    def _():
-        for src, dst in ((pd, pdt), (qg, qgt), (qu, qut)):
-            dst[...] = src[...].T
-
-    @pl.when(step < wide)
-    def _():
-        gbg[...] = scale * mm(pgt[...], dg[...])
-        gbu[...] = scale * mm(put[...], du[...])
-        gad[...] = mm(qdt[...], h[...])
-
-    @pl.when(step >= wide)
-    def _():
-        gag[...] = mm(qgt[...], x[...])
-        gau[...] = mm(qut[...], x[...])
-        gbd[...] = scale * mm(pdt[...], dy[...])
-
-
-def whole(shape):
-    return pl.BlockSpec(shape, lambda j: (0, 0), pipeline_mode=pl.Buffered(1))
-
-
-def params():
-    return pltpu.CompilerParams(dimension_semantics=('arbitrary',), vmem_limit_bytes=60 * 2 ** 20)
+def grads_body(scale, pgt_h, put_h, qdt_h, pd_h, qg_h, qu_h, x_h, dy_h, h, dg, du, gbg, gbu, gad, gag, gau, gbd,
+               lefts, flat, turned, rows_v, ins, outs, lsem, fsem, rsem, isem, xsem):
+    deep, part = ins.shape[0], ins.shape[3]
+    wide, slim = dg.shape[1] // part, x_h.shape[1] // part
+    sources, targets, tails = (dg, du, h), (gbg, gbu, gad), (gag, gau, gbd)
+
+    def span(j):
+        return pl.ds(pl.multiple_of(j * part, part), part)
+
+    def in_copy(j, i):
+        slot = lax.rem(j, deep)
+        return pltpu.make_async_copy(sources[i].at[:, span(j)], ins.at[slot, i], isem.at[slot, i])
+
+    def out_copy(dst, j, n, i):
+        slot = lax.rem(n, deep)
+        return pltpu.make_async_copy(outs.at[slot, i], dst.at[:, span(j)], xsem.at[slot, i])
+
+    left_copies = [pltpu.make_async_copy(src, lefts.at[i], lsem.at[i]) for i, src in enumerate((pgt_h, put_h, qdt_h))]
+    flat_copies = [pltpu.make_async_copy(src, flat.at[i], fsem.at[i]) for i, src in enumerate((qg_h, qu_h, pd_h))]
+    row_copies = [pltpu.make_async_copy(src, rows_v.at[i], rsem.at[i]) for i, src in enumerate((x_h, dy_h))]
+    for i in range(3):
+        left_copies[i].start()
+        in_copy(0, i).start()
+    for j in range(1, deep):
+        for i in range(3):
+            in_copy(j, i).start()
+    for copy in flat_copies + row_copies:
+        copy.start()
+    for copy in left_copies:
+        copy.wait()
+
+    def wide_step(j, carry):
+        slot = lax.rem(j, deep)
+        for i in range(3):
+            in_copy(j, i).wait()
+
+            @pl.when(j >= deep)
+            def _():
+                out_copy(targets[i], 0, j, i).wait()
+
+            vals = mm(lefts[i], ins[slot, i])
+            outs[slot, i] = vals if i == 2 else scale * vals
+            out_copy(targets[i], j, j, i).start()
+
+        @pl.when(j + deep < wide)
+        def _():
+            for i in range(3):
+                in_copy(j + deep, i).start()
+
+        return carry
+
+    lax.fori_loop(0, wide, wide_step, 0)
+    for i in range(3):
+        flat_copies[i].wait()
+        turned[i] = flat[i].T
+    for copy in row_copies:
+        copy.wait()
+
+    def slim_step(j, carry):
+        n = wide + j
+        slot = lax.rem(n, deep)
+        for i in range(3):
+            out_copy(tails[i], 0, n, i).wait()
+            vals = mm(turned[i], rows_v[i // 2, :, span(j)])
+            outs[slot, i] = scale * vals if i == 2 else vals
+            out_copy(tails[i], j, n, i).start()
+        return carry
+
+    lax.fori_loop(0, slim, slim_step, 0)
+    for n in range(deep):
+        for i in range(3):
+            out_copy(tails[i], 0, n, i).wait()
 
 
 def cost(flops, nbytes):
@@ -446,26 +518,24 @@
                 pltpu.VMEM((group, 8, 128), f32), pltpu.VMEM((group, 8, 128), f32),
                 pltpu.VMEM((6, TILE, dim), bf), pltpu.VMEM((2, 3, width, TILE), bf),
                 pltpu.VMEM((rows, dim), f32), pltpu.VMEM((rows, width), f32), pltpu.VMEM((rows, width), f32),
-                pltpu.VMEM((rows, width), bf), pltpu.VMEM((rows, width), bf), pltpu.VMEM((rows, width), bf), pltpu.VMEM((2, rows, TILE), bf),
+                pltpu.VMEM((rows, width), bf), pltpu.VMEM((rows, width), bf), pltpu.VMEM((rows, width), bf),
                 sem((chunks + 3, group)), sem((chunks + 3, group)), sem((6,)), sem((2, 3)), sem((dim // TILE, 2)), sem((2,)), sem((3,)),
             ],
             compiler_params=pltpu.CompilerParams(collective_id=0, has_side_effects=True, vmem_limit_bytes=67043328),
             cost_estimate=cost(6 * base + 6 * lora + 6 * small, 12 * dim * hidden),
             name='layer',
         )(ids_loc[None, :], x_loc, dy_loc, ag, au, bd, w_gate, w_up, w_down, bg, bu, ad)
-        steps = hidden // WIDE
-        wide_cols = pl.BlockSpec((rows, WIDE), lambda j: (0, jnp.minimum(j, steps - 1)))
-        wide_grad = pl.BlockSpec((width, WIDE), lambda j: (0, jnp.minimum(j, steps - 1)))
-        slim_cols = pl.BlockSpec((rows, TILE), lambda j: (0, jnp.maximum(j - steps, 0)))
-        slim_grad = pl.BlockSpec((width, TILE), lambda j: (0, jnp.maximum(j - steps, 0)))
         g_bg, g_bu, g_ad, g_ag, g_au, g_bd = pl.pallas_call(
-            functools.partial(grads_body, scale, steps),
-            grid=(steps + dim // TILE,),
-            in_specs=[whole((width, rows))] * 3 + [whole((rows, width))] * 3 + [slim_cols, slim_cols, wide_cols, wide_cols, wide_cols],
-            out_specs=[wide_grad, wide_grad, wide_grad, slim_grad, slim_grad, slim_grad],
+            functools.partial(grads_body, scale),
+            in_specs=[any_spec] * 11,
+            out_specs=[any_spec] * 6,
             out_shape=[arr((width, hidden), f32)] * 3 + [arr((width, dim), f32)] * 3,
-            scratch_shapes=[pltpu.VMEM((width, rows), bf)] * 3,
-            compiler_params=params(),
+            scratch_shapes=[
+                pltpu.VMEM((3, width, rows), bf), pltpu.VMEM((3, rows, width), bf), pltpu.VMEM((3, width, rows), bf), pltpu.VMEM((2, rows, dim), bf),
+                pltpu.VMEM((DEEP, 3, rows, TILE), bf), pltpu.VMEM((DEEP, 3, width, TILE), f32),
+                sem((3,)), sem((3,)), sem((2,)), sem((DEEP, 3)), sem((DEEP, 3)),
+            ],
+            compiler_params=pltpu.CompilerParams(vmem_limit_bytes=60 * 2 ** 20),
             cost_estimate=cost(3 * lora + 3 * small, 12 * width * hidden),
             name='adapter_grads',
         )(pgt, put, qdt, pd, qg, qu, x, dy, h, dg, du)

time: 180 us -> 175 us (0.972)
  Pallas kernels: 173 us -> 168 us
    pallas_call x1, Pallas kernels: 33.7 us -> 31.3 us  [device_fn(): pl.pallas_call(functools.partial(grads_body, scale), in_specs=[any_spec]...]
    pallas_call x1, Pallas kernels: 139 us -> 137 us  [device_fn(): pl.pallas_call(functools.partial(layer_body, cap, n_local, rank, scale, m...]
  transfers between devices with their start and end apart: 1 -> 1, of which waited for: 0 -> 0; matrix products, arithmetic and copies ran while one was open for 0% -> 0% of each run, Pallas kernels for 19% -> 18%
where the time goes in v3:
time: 175 us; the launch traced here: 174 us
  Pallas kernels  168 us (96%)
  starting transfers between devices  3.15 us (2%)
    pallas_call x1, Pallas kernels, device_fn(): pl.pallas_call(functools.partial(layer_body, cap, n_local, rank, scale, m...  137 us
    pallas_call x1, Pallas kernels, device_fn(): pl.pallas_call(functools.partial(grads_body, scale), in_specs=[any_spec]...  31.3 us
  transfers between devices with their start and end apart: 1, of which 0 were waited for; matrix products, arithmetic and copies ran while one was open for 0% of the time, Pallas kernels for 18%

profile of v3, /device:TPU:0, one launch (start us, length us, event | category | flops | bytes accessed | tf_op | source)
XLA Modules:
  0.0 174.3 jit_solution(11185887840747846406)
XLA Ops:
  0.6 137.1 %layer.1 = (bf16[384,2048]{1,0:T(8,128)(2,1)}, bf16[384,2048]{1,0:T(8,128)(2,1)}, bf16[384,8192]{1,0:T(8,128)(2,1)}, bf16[384,8192]{1,0:T(8,128)(2,1)}, bf16[384...) custom-call(s32[1,128]{1,0:T(1,128)} %bitcast.37, ...), custom_call_target="tpu_custom_call" | custom-call | flops 101468602368 | bytes 201326592 | tf_op jit(solution)/shard_map/layer/pallas_call | solution.py:508
  137.7 3.2 %all-to-all-start = ((bf16[8,48,2048]{2,1,0:T(8,128)(2,1)}), bf16[8,48,2048]{2,1,0:T(8,128)(2,1)S(1)}, u32[]{:S(2)}, u32[]{:S(2)}) async-start(bf16[8,48,2048]{2,1,0:T(8,128)(2,1)} %bitcast.30), calls=%async_computation | async-start | bytes 3145728 | tf_op jit(solution)/shard_map/all_to_all | solution.py:490
  140.9 0.0 copy-start.1
  140.9 0.0 copy-start
  140.9 31.3 %adapter_grads.1 = (f32[512,8192]{1,0:T(8,128)}, f32[512,8192]{1,0:T(8,128)}, f32[512,8192]{1,0:T(8,128)}, f32[512,2048]{1,0:T(8,128)}, f32[512,2048]{1,0:T(8,128)}, /*index=5*/f32[512,2048]{1,0:T(8,128)}) custom-call(bf16[512,384]{1,0:T(8,128)(2,1)} %get-tuple-element.31.pgt_h, bf16[512,384]{1,0:T(8,128)(2,1)} %get-tuple-element.32.put_h, ...), custom_call_target="tpu_custom_call" | custom-call | flops 12079595520 | bytes 50331648 | tf_op jit(solution)/shard_map/adapter_grads/pallas_call | solution.py:528
  172.2 0.0 all-to-all-done
  172.2 0.0 copy-done.1
  172.2 1.3 convolution_convert_fusion
  173.5 0.0 copy-done
  173.5 0.8 copy.21
Async XLA Ops:
  137.7 34.5 %all-to-all-start = ((bf16[8,48,2048]{2,1,0:T(8,128)(2,1)}), bf16[8,48,2048]{2,1,0:T(8,128)(2,1)S(1)}, u32[]{:S(2)}, u32[]{:S(2)}) async-start(bf16[8,48,2048]{2,1,0:T(8,128)(2,1)} %bitcast.30), calls=%async_computation | async-start | bytes 3145728 | tf_op jit(solution)/shard_map/all_to_all | solution.py:490
  140.9 31.3 %copy-start.1 = (bf16[384,128]{1,0:T(8,128)(2,1)S(1)}, bf16[384,128]{1,0:T(8,128)(2,1)}, u32[]{:S(2)}) copy-start(bf16[384,128]{1,0:T(8,128)(2,1)} %get-tuple-element.29) | copy-start | bytes 294916
  140.9 32.6 %copy-start = (bf16[128,2048]{1,0:T(8,128)(2,1)S(1)}, bf16[128,2048]{1,0:T(8,128)(2,1)}, u32[]{:S(2)}) copy-start(bf16[128,2048]{1,0:T(8,128)(2,1)} %get-tuple-element.56) | copy-start | bytes 1572868

commit v4 on v3

--- a/solution.py
+++ b/solution.py
@@ -9,7 +9,7 @@
 
 LORA_ALPHA = 32
 TILE = 512
-DEEP = 4
+DEEP = 6
 f32 = jnp.float32
 bf = jnp.bfloat16
 
@@ -27,12 +27,12 @@
     return jnp.where(cols == ids, vals, 0.0).astype(bf)
 
 
-def layer_body(cap, n_local, rank, scale, axes, ids_r, x_loc, dy_loc, ag_h, au_h, bd_h, wg, wu, wd, bg, bu, ad,
+def layer_body(cap, n_local, rank, scale, axes, ids_r, x_in, dy_in, ag_h, au_h, bd_h, wg, wu, wd, bg, bu, ad,
                x_o, dy_o, h_o, dg_o, du_o, dx_o, out_o, pack_o, pgt_o, put_o, qdt_o, pd_o, qg_o, qu_o,
-               gu, x_own, dy_own, xs, dys, out_v, ids_s, ids_v, wbuf, bbuf, acc, qa, qb, pg, pu, qd,
+               gu, x_own, dy_own, xs, dys, out_v, ids_s, ids_v, wbuf, bbuf, acc, qa, qb, pg, pu,
                send_sem, recv_sem, wsem, bsem, gsem, hsem, osem):
-    group, dim = ids_s.shape[0], x_loc.shape[1]
-    tokens, hidden = x_loc.shape[0], wg.shape[1]
+    group, dim = ids_s.shape[0], x_in.shape[1]
+    tokens, hidden = x_in.shape[0], wg.shape[1]
     rows = group * cap
     n_slots, part = wbuf.shape[0], wbuf.shape[1]
     chunks = dim // part
@@ -88,6 +88,10 @@
             for i in which:
                 adapter_copy(0, ii, i).wait()
 
+    x_loc, dy_loc = out_v.at[pl.ds(0, tokens)], out_v.at[pl.ds(tokens, tokens)]
+    in_copies = [pltpu.make_async_copy(src, dst, osem.at[i]) for i, (src, dst) in enumerate(((x_in, x_loc), (dy_in, dy_loc)))]
+    for copy in in_copies:
+        copy.start()
     start_pair(0, 0, 0)
     start_pair(2, 0, 1)
     for j in range(2):
@@ -103,10 +107,6 @@
     pack = jnp.where(lax.broadcasted_iota(jnp.int32, (rows, tokens), 0) == owner * cap + rank_in, 1.0, 0.0).astype(bf)
     pack_o[...] = pack
     lanes = 128
-    spread = jnp.where(lax.broadcasted_iota(jnp.int32, (group * lanes, tokens), 0) == owner * lanes + rank_in, 1.0, 0.0).astype(bf)
-    tagged = mm(jnp.broadcast_to((local + 1).astype(f32), (8, tokens)).astype(bf), spread, 1, 1)
-    for d in range(group):
-        ids_s[d] = tagged[:, d * lanes:(d + 1) * lanes]
 
     def pack_part(src, dst, c):
         span = slice(c * part, (c + 1) * part)
@@ -131,6 +131,7 @@
     id_copies = [id_copy(k) for k in others]
     out_copies = [row_copy(xs, out_v, pl.ds(0, dim), chunks + 2, k) for k in others]
 
+    in_copies[0].wait()
     pack_part(x_loc, xs, 0)
     pl.semaphore_wait(barrier, group - 1)
     for c in range(chunks):
@@ -138,8 +139,13 @@
             pack_part(x_loc, xs, c + 1)
         for copy in x_copies[c]:
             copy.start()
+    spread = jnp.where(lax.broadcasted_iota(jnp.int32, (group * lanes, tokens), 0) == owner * lanes + rank_in, 1.0, 0.0).astype(bf)
+    tagged = mm(jnp.broadcast_to((local + 1).astype(f32), (8, tokens)).astype(bf), spread, 1, 1)
+    for d in range(group):
+        ids_s[d] = tagged[:, d * lanes:(d + 1) * lanes]
     for copy in id_copies:
         copy.start()
+    in_copies[1].wait()
     for c in range(chunks):
         pack_part(dy_loc, dys, c)
     x_own[mine, :] = xs[mine, :]
@@ -170,22 +176,20 @@
 
         def pre_step(i, carry, last_step=False):
             p = c * across + 2 * i
+            t = 2 * p
             if last_step:
                 start_tile(2 * pairs, ag_h)
                 start_tile(2 * pairs + 1, au_h)
+                start_down(2 * pairs + 2, 0)
+                start_down(2 * pairs + 3, 1)
             else:
                 ahead(p + 2)
+                ahead(p + 3)
+            slots = [wait_tile(t + n) for n in range(4)]
             for half in range(2):
-                t = 2 * (p + half)
                 span = aligned((2 * i + half) * dim, dim, dim)
-                one, two = wait_tile(t), wait_tile(t + 1)
-                gu[0, :, span] += mm(x_own[:, c * part:(c + 1) * part], wbuf[one])
-                gu[1, :, span] += mm(x_own[:, c * part:(c + 1) * part], wbuf[two])
-                if half == 0 and last_step:
-                    start_down(2 * pairs + 2, 0)
-                    start_down(2 * pairs + 3, 1)
-                elif half == 0:
-                    ahead(p + 3)
+                gu[0, :, span] += mm(x_own[:, c * part:(c + 1) * part], wbuf[slots[2 * half]])
+                gu[1, :, span] += mm(x_own[:, c * part:(c + 1) * part], wbuf[slots[2 * half + 1]])
             return carry
 
         turns = across // 2
@@ -274,9 +278,11 @@
             copy.wait_send()
     slot = wait_tile(base)
     pd = keep(qa[...], ids_col, rank)
-    pd_o[...] = pd
+    pg[...] = pd
+    pd_out = pltpu.make_async_copy(pg, pd_o, osem.at[3])
+    pd_out.start()
     xs[...] = (x_own[...].astype(f32) + acc[...] + rounded(scale * mm(pd, wbuf[slot]))).astype(bf)
-    qd[...] = keep(scale * mm(dy_own[...], wbuf[slot], 1, 1), ids_col, rank)
+    pu[...] = keep(scale * mm(dy_own[...], wbuf[slot], 1, 1), ids_col, rank)
     for copy in out_copies:
         copy.start()
     out_v[mine, :] = xs[mine, :]
@@ -316,12 +322,12 @@
                 gate, up = gu[0, :, span], gu[1, :, span]
                 sig = jax.nn.sigmoid(gate)
                 act = gate * sig
-                dh = mm(dy_own[...], wbuf[slots[ii]], 1, 1) + rounded(mm(qd[...], bbuf[ii, 2]))
+                dh = mm(dy_own[...], wbuf[slots[ii]], 1, 1) + rounded(mm(pu[...], bbuf[ii, 2]))
                 x_own[:, here] = (dh * up * sig * (1.0 + gate * (1.0 - sig))).astype(bf)
                 dys[:, here] = (dh * act).astype(bf)
             refill(j0, (2,))
             slab = aligned(lax.rem(lax.div(j0, 2), width // lanes) * lanes, lanes, lanes)
-            qdt_o[slab, :] = qd[:, slab].T
+            qdt_o[slab, :] = pu[:, slab].T
             wait_adapters((0, 1))
             for ii in range(2):
                 here = aligned((i0 + ii) * part, part, part)
@@ -335,14 +341,12 @@
         lax.fori_loop(0, per // 2, sub_step, 0)
 
         for turn in range(per // 2):
-            final = turn == per // 2 - 1
             t0 = first + per + 4 * turn
-            nxt = jnp.minimum((s + 1) * per, steps - per)
-            if final:
+            if turn == per // 2 - 1:
                 @pl.when(s < across - 1)
                 def _():
-                    start_down(t0 + 4, nxt)
-                    start_down(t0 + 5, nxt + 1)
+                    for n in range(4):
+                        start_down(t0 + 4 + n, (s + 1) * per + n)
 
                 @pl.when(s == across - 1)
                 def _():
@@ -350,29 +354,26 @@
                     start_tile(t0 + 5, au_h)
             else:
                 start_pair(t0 + 4, 2 * turn + 2, s)
+                start_pair(t0 + 6, 2 * turn + 3, s)
+            slots = [wait_tile(t0 + n) for n in range(4)]
             for half in range(2):
                 d = 2 * turn + half
-                t = t0 + 2 * half
                 here = slice(d * part, (d + 1) * part)
-                one, two = wait_tile(t), wait_tile(t + 1)
-                acc[:, here] += mm(x_own[...], wbuf[one], 1, 1) + mm(dys[...], wbuf[two], 1, 1)
-                if half == 0 and final:
-                    start_down(t0 + 6, nxt + 2)
-                    start_down(t0 + 7, nxt + 3)
-                elif half == 0:
-                    start_pair(t0 + 6, 2 * turn + 3, s)
+                acc[:, here] += mm(x_own[...], wbuf[slots[2 * half]], 1, 1) + mm(dys[...], wbuf[slots[2 * half + 1]], 1, 1)
         return carry
 
     lax.fori_loop(0, across, super_step, 0)
     base += across * width_tiles
     one, two = wait_tile(base), wait_tile(base + 1)
-    wait_tile(base + 2)
-    wait_tile(base + 3)
     wait_adapters((0, 1, 2))
     qg = keep(scale * qa[...], ids_col, rank)
     qu = keep(scale * qb[...], ids_col, rank)
-    qg_o[...] = qg
-    qu_o[...] = qu
+    pd_out.wait()
+    pg[...] = qg
+    pu[...] = qu
+    q_outs = [pltpu.make_async_copy(src, dst, osem.at[3 + i]) for i, (src, dst) in enumerate(((pg, qg_o), (pu, qu_o)))]
+    for copy in q_outs:
+        copy.start()
     lora = rounded(mm(qg, wbuf[one]) + mm(qu, wbuf[two]))
     for i in range(per):
         for copy in grad_copies(0, i):
@@ -388,6 +389,8 @@
             copy.wait_send()
     dy_out.wait()
     dx_out.wait()
+    for copy in q_outs:
+        copy.wait()
 
 
 def grads_body(scale, pgt_h, put_h, qdt_h, pd_h, qg_h, qu_h, x_h, dy_h, h, dg, du, gbg, gbu, gad, gag, gau, gbd,
@@ -421,27 +424,34 @@
     for copy in left_copies:
         copy.wait()
 
-    def wide_step(j, carry):
-        slot = lax.rem(j, deep)
-        for i in range(3):
-            in_copy(j, i).wait()
-
-            @pl.when(j >= deep)
-            def _():
-                out_copy(targets[i], 0, j, i).wait()
-
-            vals = mm(lefts[i], ins[slot, i])
-            outs[slot, i] = vals if i == 2 else scale * vals
-            out_copy(targets[i], j, j, i).start()
+    def wide_step(jj, carry):
+        j = 2 * jj
+        for n in range(2):
+            for i in range(3):
+                in_copy(j + n, i).wait()
+
+        @pl.when(j >= deep)
+        def _():
+            for n in range(2):
+                for i in range(3):
+                    out_copy(targets[i], 0, j + n, i).wait()
+
+        for n in range(2):
+            slot = lax.rem(j + n, deep)
+            for i in range(3):
+                vals = mm(lefts[i], ins[slot, i])
+                outs[slot, i] = vals if i == 2 else scale * vals
+                out_copy(targets[i], j + n, j + n, i).start()
 
         @pl.when(j + deep < wide)
         def _():
-            for i in range(3):
-                in_copy(j + deep, i).start()
+            for n in range(2):
+                for i in range(3):
+                    in_copy(j + n + deep, i).start()
 
         return carry
 
-    lax.fori_loop(0, wide, wide_step, 0)
+    lax.fori_loop(0, wide // 2, wide_step, 0)
     for i in range(3):
         flat_copies[i].wait()
         turned[i] = flat[i].T
@@ -507,8 +517,8 @@
         sem = pltpu.SemaphoreType.DMA
         x, dy, h, dg, du, dx, out, pack, pgt, put, qdt, pd, qg, qu = pl.pallas_call(
             functools.partial(layer_body, cap, n_local, rank, scale, mesh.axis_names),
-            in_specs=[vmem_spec] * 3 + [any_spec] * 9,
-            out_specs=[any_spec] * 6 + [vmem_spec] * 8,
+            in_specs=[vmem_spec] + [any_spec] * 11,
+            out_specs=[any_spec] * 6 + [vmem_spec] * 5 + [any_spec] * 3,
             out_shape=[arr((rows, dim), bf)] * 2 + [arr((rows, hidden), bf)] * 3 + [arr((rows, dim), bf), arr((tokens, dim), bf), arr((rows, tokens), bf)]
             + [arr((width, rows), bf)] * 3 + [arr((rows, width), bf)] * 3,
             scratch_shapes=[
@@ -516,10 +526,10 @@
                 pltpu.VMEM((rows, dim), bf), pltpu.VMEM((rows, dim), bf), pltpu.VMEM((rows, dim), bf), pltpu.VMEM((rows, dim), bf),
                 pltpu.VMEM((rows, dim), bf),
                 pltpu.VMEM((group, 8, 128), f32), pltpu.VMEM((group, 8, 128), f32),
-                pltpu.VMEM((6, TILE, dim), bf), pltpu.VMEM((2, 3, width, TILE), bf),
+                pltpu.VMEM((8, TILE, dim), bf), pltpu.VMEM((2, 3, width, TILE), bf),
                 pltpu.VMEM((rows, dim), f32), pltpu.VMEM((rows, width), f32), pltpu.VMEM((rows, width), f32),
-                pltpu.VMEM((rows, width), bf), pltpu.VMEM((rows, width), bf), pltpu.VMEM((rows, width), bf),
-                sem((chunks + 3, group)), sem((chunks + 3, group)), sem((6,)), sem((2, 3)), sem((dim // TILE, 2)), sem((2,)), sem((3,)),
+                pltpu.VMEM((rows, width), bf), pltpu.VMEM((rows, width), bf),
+                sem((chunks + 3, group)), sem((chunks + 3, group)), sem((8,)), sem((2, 3)), sem((dim // TILE, 2)), sem((2,)), sem((5,)),
             ],
             compiler_params=pltpu.CompilerParams(collective_id=0, has_side_effects=True, vmem_limit_bytes=67043328),
             cost_estimate=cost(6 * base + 6 * lora + 6 * small, 12 * dim * hidden),

time: 175 us -> 171 us (0.977)
  Pallas kernels: 168 us -> 165 us
    pallas_call x1, Pallas kernels: 31.3 us -> 28.3 us  [device_fn(): pl.pallas_call(functools.partial(grads_body, scale), in_specs=[any_spec]...]
  transfers between devices with their start and end apart: 1 -> 1, of which waited for: 0 -> 0; matrix products, arithmetic and copies ran while one was open for 0% -> 0% of each run, Pallas kernels for 18% -> 17%
where the time goes in v4:
time: 171 us; the launch traced here: 170 us
  Pallas kernels  165 us (96%)
  starting transfers between devices  2.59 us (2%)
    pallas_call x1, Pallas kernels, device_fn(): pl.pallas_call(functools.partial(layer_body, cap, n_local, rank, scale, m...  137 us
    pallas_call x1, Pallas kernels, device_fn(): pl.pallas_call(functools.partial(grads_body, scale), in_specs=[any_spec]...  28.3 us
  transfers between devices with their start and end apart: 1, of which 0 were waited for; matrix products, arithmetic and copies ran while one was open for 0% of the time, Pallas kernels for 17%

profile of v4, /device:TPU:0, one launch (start us, length us, event | category | flops | bytes accessed | tf_op | source)
XLA Modules:
  0.0 170.2 jit_solution(10718587251735535866)
XLA Ops:
  0.6 136.5 %layer.1 = (bf16[384,2048]{1,0:T(8,128)(2,1)}, bf16[384,2048]{1,0:T(8,128)(2,1)}, bf16[384,8192]{1,0:T(8,128)(2,1)}, bf16[384,8192]{1,0:T(8,128)(2,1)}, bf16[384...) custom-call(s32[1,128]{1,0:T(1,128)} %bitcast.37, ...), custom_call_target="tpu_custom_call" | custom-call | flops 101468602368 | bytes 201326592 | tf_op jit(solution)/shard_map/layer/pallas_call | solution.py:518
  137.2 2.6 %all-to-all-start = ((bf16[8,48,2048]{2,1,0:T(8,128)(2,1)}), bf16[8,48,2048]{2,1,0:T(8,128)(2,1)S(1)}, u32[]{:S(2)}, u32[]{:S(2)}) async-start(bf16[8,48,2048]{2,1,0:T(8,128)(2,1)} %bitcast.30), calls=%async_computation | async-start | bytes 3145728 | tf_op jit(solution)/shard_map/all_to_all | solution.py:500
  139.8 0.0 copy-start.1
  139.8 0.0 copy-start
  139.8 28.3 %adapter_grads.1 = (f32[512,8192]{1,0:T(8,128)}, f32[512,8192]{1,0:T(8,128)}, f32[512,8192]{1,0:T(8,128)}, f32[512,2048]{1,0:T(8,128)}, f32[512,2048]{1,0:T(8,128)}, /*index=5*/f32[512,2048]{1,0:T(8,128)}) custom-call(bf16[512,384]{1,0:T(8,128)(2,1)} %get-tuple-element.31.pgt_h, bf16[512,384]{1,0:T(8,128)(2,1)} %get-tuple-element.32.put_h, ...), custom_call_target="tpu_custom_call" | custom-call | flops 12079595520 | bytes 50331648 | tf_op jit(solution)/shard_map/adapter_grads/pallas_call | solution.py:538
  168.1 0.0 all-to-all-done
  168.1 0.0 copy-done.1
  168.2 1.3 convolution_convert_fusion
  169.4 0.0 copy-done
  169.4 0.8 copy.21
Async XLA Ops:
  137.2 31.0 %all-to-all-start = ((bf16[8,48,2048]{2,1,0:T(8,128)(2,1)}), bf16[8,48,2048]{2,1,0:T(8,128)(2,1)S(1)}, u32[]{:S(2)}, u32[]{:S(2)}) async-start(bf16[8,48,2048]{2,1,0:T(8,128)(2,1)} %bitcast.30), calls=%async_computation | async-start | bytes 3145728 | tf_op jit(solution)/shard_map/all_to_all | solution.py:500
  139.8 28.4 %copy-start.1 = (bf16[384,128]{1,0:T(8,128)(2,1)S(1)}, bf16[384,128]{1,0:T(8,128)(2,1)}, u32[]{:S(2)}) copy-start(bf16[384,128]{1,0:T(8,128)(2,1)} %get-tuple-element.29) | copy-start | bytes 294916
  139.8 29.7 %copy-start = (bf16[128,2048]{1,0:T(8,128)(2,1)S(1)}, bf16[128,2048]{1,0:T(8,128)(2,1)}, u32[]{:S(2)}) copy-start(bf16[128,2048]{1,0:T(8,128)(2,1)} %get-tuple-element.56) | copy-start | bytes 1572868
